TPU v7x, 256 devices: a whole 4x4x8 slice. The times are simulated.
256 devices in a mesh: rep: 1, dp: 256 (over x, y, z, core).
Axes of the slice: x: 4, y: 4, z: 8, core: 2. Of those that a mesh axis runs over, the one named last changes fastest.
Arguments:
- x: bfloat16 [256, 1024, 1536], P(('rep', 'dp'))
- dy: bfloat16 [256, 1024, 1536], P(('rep', 'dp'))
- w_gate: bfloat16 [2, 1536, 3584], replicated
- w_up: bfloat16 [2, 1536, 3584], replicated
- w_down: bfloat16 [2, 3584, 1536], replicated
- m_w_gate: float32 [2, 1536, 3584], P(None, 'dp')
- m_w_up: float32 [2, 1536, 3584], P(None, 'dp')
- m_w_down: float32 [2, 3584, 1536], P(None, 'dp')
- v_w_gate: float32 [2, 1536, 3584], P(None, 'dp')
- v_w_up: float32 [2, 1536, 3584], P(None, 'dp')
- v_w_down: float32 [2, 3584, 1536], P(None, 'dp')
Outputs:
- output 1: bfloat16 [2, 1536, 3584], P('rep')
- output 2: bfloat16 [2, 1536, 3584], P('rep')
- output 3: bfloat16 [2, 3584, 1536], P('rep')
- output 4: float32 [2, 1536, 3584], P('rep', 'dp')
- output 5: float32 [2, 1536, 3584], P('rep', 'dp')
- output 6: float32 [2, 3584, 1536], P('rep', 'dp')
- output 7: float32 [2, 1536, 3584], P('rep', 'dp')
- output 8: float32 [2, 1536, 3584], P('rep', 'dp')
- output 9: float32 [2, 3584, 1536], P('rep', 'dp')
All inputs are finite; a program needn't handle non-finite values.
Results may differ from a plain program's by a relative error of at most 0.022.
Values are sent between devices in bfloat16 or wider.
A program may use at most 768 MiB of HBM per device.

v0:
```python
import functools
import jax, jax.numpy as jnp
from jax import lax
from jax.experimental import pallas as pl
from jax.experimental.pallas import tpu as pltpu

bf16, f32 = jnp.bfloat16, jnp.float32
MATS = 6
UNIT = (24, 896)
DOWN = (56, 384)
TILE = (8, 128)
PADS = (8, 16)
ORDERS = ("xyz", "yzx", "zxy")
COLUMNS = ((0, 384), (384, 256), (640, 256))
KINDS = ("s", "f", "z", "d", "e")
SCATTER_TIMES, SCATTER_STEP = "#:LMWbb{'6CCMMXaajjs#/'85CTT]ghq", 18
GATHER_TIMES, GATHER_STEPS = '#-.4799Yj~#337;<DEOPQ_oi#((3@AAKX\\bgoy', (4, 14)
MESH = pl.DeviceIdType.MESH
START, MORE = 0, 1
NORTH, SOUTH = 0, 1


def time_of(character):
    return ord(character) - ord("#")


class Torus:
    def __init__(self, dims):
        self.dims = dict(zip("xyz", dims))
        self.cores = 2
        _, Y, Z = dims
        self.stride = dict(zip("xyz", (Y * Z * self.cores, Z * self.cores, self.cores)))
        self.rep, self.idx = lax.axis_index("rep"), lax.axis_index("dp")
        self.at = {d: lax.rem(lax.div(self.idx, self.stride[d]), self.dims[d]) for d in "xyz"}
        self.core = lax.rem(self.idx, self.cores)

    def wrap(self, d, value):
        n = self.dims[d]
        return lax.rem(value + n, n)

    def beside(self, d, offset):
        return (self.rep, self.idx + (self.wrap(d, self.at[d] + offset) - self.at[d]) * self.stride[d])

    def partner(self):
        return (self.rep, self.idx + 1 - 2 * self.core)

    def everyone(self):
        return [self.beside(d, o) for d in "xyz" for o in range(1, self.dims[d])]

    def group(self, s):
        return (self.rep, self.idx - lax.rem(self.idx, 4) + s)

    def enter(self):
        me = lax.rem(self.idx, 4)
        barrier = pltpu.get_barrier_semaphore()
        devices = self.everyone() + [self.partner(), self.group(lax.rem(me + 3 - 2 * self.core, 4))]
        for device in devices:
            signal(barrier, device)
        pl.semaphore_wait(barrier, len(devices))


def signal(sem, device):
    pl.semaphore_signal(sem, inc=1, device_id=device, device_id_type=MESH)


def remote(src, dst, send, recv, device):
    return pltpu.make_async_remote_copy(src_ref=src, dst_ref=dst, send_sem=send, recv_sem=recv, device_id=device, device_id_type=MESH)


class Ring:
    def __init__(self, color, phase, d, n):
        self.name = f"{color.k}{phase}"
        self.color, self.phase, self.d, self.n = color, phase, d, n
        self.steps = (n // 2, (n - 1) // 2)
        self.sides = [side for side in (NORTH, SOUTH) if self.steps[side]]

    def message(self, side, m):
        return m + side * self.steps[NORTH]


class Color:
    def __init__(self, k, dims):
        self.k, self.order = k, ORDERS[k]
        start, self.width = COLUMNS[k]
        self.columns = pl.ds(start, self.width)
        size = dict(zip("xyz", dims))
        n = [size[d] for d in self.order]
        self.rings = [Ring(self, phase, d, m) for phase, (d, m) in enumerate(zip(self.order, n))]
        first, second, third = self.order
        self.rest = [d for d in "xyz" if d != first]
        self.block = (tuple(size[d] for d in self.rest), (size[third],))
        self.unit = (UNIT[0], self.width)

    def index(self, **at):
        return tuple(at.get(d, slice(None)) for d in "xyz")

    def within(self, b):
        return tuple(b if d == self.order[1] else slice(None) for d in self.rest)

    def events(self, gather):
        rings, direct = [], [("d", self, 2, START, START), ("e", self, 2, START, START)]
        for ring in self.rings[:2][:: -1 if gather else 1]:
            rings.append(("s", self, ring.phase, START, START))
            for j in range(1, ring.steps[NORTH] + gather):
                rings += [("f", self, ring.phase, side, j) for side in (NORTH, SOUTH) if side == NORTH or j < ring.steps[SOUTH] + gather]
            if not gather:
                rings.append(("z", self, ring.phase, START, START))
        return direct + rings if gather else rings + direct


def add_blocks(dst, dst_index, terms, shape):
    def at(ref, index, place):
        place = list(place)
        return ref[tuple([place.pop(0) if isinstance(e, slice) else e for e in index] + place)]

    def row(i, _):
        for rest in [(j,) for n in shape[1:] for j in range(n)] or [()]:
            place = (i, *rest)
            dst[(*dst_index, *place)] = sum(at(ref, index, place).astype(f32) for ref, index in terms).astype(dst.dtype)
        return 0

    lax.fori_loop(0, shape[0], row, 0)


def direct(t, ring, o, w, src, dst, s, slot, half):
    name = ring.name
    return remote(src, dst, s["send" + name].at[half, o - 1], s["recv" + name].at[slot, o - 1], t.beside(ring.d, o))


class Scatter:
    def __init__(self, dims):
        self.colors = [Color(k, dims) for k in range(len(ORDERS))]
        events = [e for c in self.colors for e in c.events(False)]
        times = [time_of(c) for c in SCATTER_TIMES]
        order = sorted(range(len(events)), key=lambda i: (times[i] % SCATTER_STEP, i))
        self.order = [(events[i], times[i] // SCATTER_STEP) for i in order]
        self.depth = max(lag for _, lag in self.order)
        self.slots = self.depth + 1
        ends = [i for i, (e, lag) in enumerate(self.order) if e[0] == "e"]
        self.last = max(ends, key=lambda i: (self.order[i][1], i))
        self.first = min(i for i, (e, lag) in enumerate(self.order) if e[0] == "s" and not e[2])

    def scratch(self):
        shapes = {}
        NS = self.slots
        for c in self.colors:
            for ring in c.rings:
                n, name = ring.n, ring.name
                block = (c.block + ((),))[ring.phase] + c.unit
                shapes["recv" + name] = pltpu.SemaphoreType.DMA((NS, n - 1))
                shapes["send" + name] = pltpu.SemaphoreType.DMA((NS, n - 1))
                shapes["in" + name] = pltpu.VMEM((NS, n - 1) + block, bf16)
                shapes["out" + name] = pltpu.VMEM((self.kept(c, ring.phase, "s" if ring.phase < 2 else "d"), len(ring.sides) if ring.phase < 2 else n - 1) + block, bf16)
                if ring.phase < 2:
                    shapes["sum" + name] = pltpu.VMEM((self.kept(c, ring.phase, "z"),) + block, f32)
            n = c.rings[0].n
            shapes[f"load{c.k}"] = pltpu.VMEM((n, 2) + c.block[0] + c.unit, bf16)
            shapes[f"load_sem{c.k}"] = pltpu.SemaphoreType.DMA((n, 2))
        shapes["part_send"] = pltpu.SemaphoreType.DMA((MATS,))
        shapes["part_recv"] = pltpu.SemaphoreType.DMA((MATS,))
        shapes["free"] = pltpu.SemaphoreType.REGULAR((MATS,))
        return shapes

    def lags(self, c, phase, kinds):
        return [lag for e, lag in self.order if e[1] is c and e[2] == phase and e[0] in kinds]

    def kept(self, c, phase, kind):
        if kind == "s":
            ends = self.lags(c, phase, "z")
        elif kind == "d":
            ends = self.lags(c, phase, "e")
        else:
            ends = self.lags(c, phase + 1, "ze")
        return max(ends) - min(self.lags(c, phase, kind)) + 1

    def bind(self, torus, g, pg, unit, s):
        self.t, self.g, self.pg, self.unit, self.s = torus, g, pg, unit, s

    def partner_copy(self, w):
        t = self.t
        return remote(self.g.at[w, :, :, :, 1 - t.core], self.pg.at[w], self.s["part_send"].at[w], self.s["part_recv"].at[w], t.partner())

    def sign(self, side, w):
        return (1 - 2 * lax.rem(w, 2)) * (1 - 2 * side)

    def target(self, ring, side, j, w):
        return self.t.wrap(ring.d, self.t.at[ring.d] + self.sign(side, w) * (ring.steps[side] - j))

    def loads(self, c, side, j, w):
        ring = c.rings[0]
        place = ring.message(side, j) if j < ring.steps[side] else ring.n - 1
        index = c.index(**{ring.d: self.target(ring, side, j, w)})
        columns = (slice(None), c.columns)
        buf, sem = self.s[f"load{c.k}"], self.s[f"load_sem{c.k}"]
        sources = self.g.at[(w, *index, self.t.core, *columns)], self.pg.at[(w, *index, *columns)]
        return [pltpu.make_async_copy(source, buf.at[place, n], sem.at[place, n]) for n, source in enumerate(sources)]

    def start_loads(self, w):
        for c in self.colors:
            ring = c.rings[0]
            for side in ring.sides:
                for j in range(ring.steps[side] + (side == NORTH)):
                    for copy in self.loads(c, side, j, w):
                        copy.start()

    def message(self, ring, side, m, w, src):
        s, name = self.s, ring.name
        n, slot = ring.message(side, m), lax.rem(w, self.slots)
        return remote(src, s["in" + name].at[slot, n], s["send" + name].at[slot, n], s["recv" + name].at[slot, n], self.t.beside(ring.d, self.sign(side, w)))

    def add(self, dst, index, ring, side, j, w, terms):
        c, s = ring.color, self.s
        if ring.phase:
            before = s["sum" + c.rings[0].name]
            own = [(before, (lax.rem(w, before.shape[0]), *c.within(self.target(ring, side, j, w))))]
        else:
            place = ring.message(side, j) if j < ring.steps[side] else ring.n - 1
            for copy in self.loads(c, side, j, w):
                copy.wait()
            own = [(s[f"load{c.k}"], (place, n)) for n in range(2)]
        add_blocks(dst, index, own + terms, c.block[ring.phase])
        if not ring.phase:

            @pl.when(w + 1 < MATS)
            def _():
                for copy in self.loads(c, side, j, w + 1):
                    copy.start()

    def event(self, kind, c, phase, side, j, w):
        ring, s = c.rings[phase], self.s
        name, slot = ring.name, lax.rem(w, self.slots)
        box, out = s["in" + name], s["out" + name]
        part = lax.rem(w, out.shape[0])
        if kind == "s":
            for side in ring.sides:
                self.add(out, (part, side), ring, side, 0, w, [])
                self.message(ring, side, 0, w, out.at[part, side]).start()
        elif kind == "f":
            at = (slot, ring.message(side, j - 1))
            self.message(ring, side, j - 1, w, out.at[part, 0]).wait_recv()
            self.add(box, at, ring, side, j, w, [(box, at)])
            self.message(ring, side, j, w, box.at[at]).start()
        elif kind == "z":
            terms = []
            for side in ring.sides:
                m = ring.steps[side] - 1
                self.message(ring, side, m, w, out.at[part, 0]).wait_recv()
                terms.append((box, (slot, ring.message(side, m))))
            total = s["sum" + name]
            self.add(total, (lax.rem(w, total.shape[0]),), ring, NORTH, ring.steps[NORTH], w, terms)
            for side in ring.sides:
                for m in range(ring.steps[side]):
                    self.message(ring, side, m, w, out.at[part, 0]).wait_send()
        else:
            total = s["sum" + c.rings[1].name]
            last = lax.rem(w, total.shape[0])
            copies = [direct(self.t, ring, o, w, out.at[part, o - 1], box.at[slot, o - 1], s, slot, slot) for o in range(1, ring.n)]
            if kind == "d":
                for o, copy in enumerate(copies):
                    out[part, o] = total[last, self.t.wrap(ring.d, self.t.at[ring.d] + o + 1)].astype(bf16)
                    copy.start()
            else:
                value = total[last, self.t.at[ring.d]]
                for o, copy in enumerate(copies):
                    copy.wait_recv()
                    value = value + box[slot, o].astype(f32)
                self.unit[w, :, c.columns] = value
                for copy in copies:
                    copy.wait_send()

    def step(self, i):
        @pl.when(i + 1 < MATS)
        def _():
            self.partner_copy(i + 1).wait_recv()

        for n, (e, lag) in enumerate(self.order):
            w = i - lag

            @pl.when((w >= 0) & (w < MATS))
            def _():
                if n == self.first:

                    @pl.when(w >= self.slots)
                    def _():
                        pl.semaphore_wait(self.s["free"].at[w - self.slots], len(self.t.everyone()))

                self.event(*e, w)
                if n == self.last:

                    @pl.when(w + self.slots < MATS)
                    def _():
                        for device in self.t.everyone():
                            signal(self.s["free"].at[w], device)

    def run(self):
        for w in range(MATS):
            self.partner_copy(w).start()
        self.partner_copy(0).wait_recv()
        self.start_loads(0)

        def body(i, _):
            self.step(i)
            return 0

        lax.fori_loop(0, MATS + self.depth, body, 0)
        for w in range(MATS):
            self.partner_copy(w).wait_send()


WAVES = ((1, 1), (0, 1), (0, 3), (1, 0), (0, 0), (0, 2))
SHAPES = (UNIT, DOWN)


def tiles(R, C):
    r, c = TILE
    across, wide = C // c, UNIT[1] // c
    for n in range(R * C // (r * c)):
        yield (pl.ds(n // across * r, r), pl.ds(n % across * c, c)), (pl.ds(n // wide * r, r), pl.ds(n % wide * c, c))


def exchange_scratch():
    shapes = {}
    for kind, (R, C) in enumerate(SHAPES):
        n = sum(w[0] == kind for w in WAVES)
        shapes[f"nat{kind}"] = pltpu.VMEM((R, C), f32)
        shapes[f"slab{kind}"] = pltpu.VMEM((4, n, PADS[kind], C), bf16)
        shapes[f"rows{kind}"] = pltpu.VMEM((4, n, PADS[kind], C), bf16)
    shapes["x_send"] = pltpu.SemaphoreType.DMA((2, 4))
    shapes["x_recv"] = pltpu.SemaphoreType.DMA((2, 4))
    return shapes


def exchange(t, s):
    me = lax.rem(t.idx, 4)
    copies = []
    for o in range(1, 4):
        to = lax.rem(me + o, 4)
        for kind in range(2):
            copies.append(remote(s[f"slab{kind}"].at[to], s[f"rows{kind}"].at[me], s["x_send"].at[kind, o], s["x_recv"].at[kind, o], t.group(to)))
    for copy in copies:
        copy.start()
    for kind in range(2):
        s[f"rows{kind}"][me] = s[f"slab{kind}"][me]
    for copy in copies:
        copy.wait()


def scatter_kernel(dims, names, g, *refs):
    outs, pg, s = refs[:2], refs[2], dict(zip(names, refs[3:], strict=True))
    t = Torus(dims)
    t.enter()
    sc = Scatter(dims)
    sc.bind(t, g, pg, s["unit"], s)
    sc.run()
    for w, (kind, at) in enumerate(WAVES):
        R, C = SHAPES[kind]
        nat, slab = s[f"nat{kind}"], s[f"slab{kind}"]
        for natural, unit in tiles(R, C):
            nat[natural] = s["unit"][(w, *unit)]
        rows = R // 4
        for q in range(4):
            slab[q, at, 0:rows, :] = nat[q * rows : (q + 1) * rows, :].astype(bf16)
    exchange(t, s)
    for kind, out in enumerate(outs):
        C = SHAPES[kind][1]
        for q in range(4):
            out[:, :, C * q : C * (q + 1)] = s[f"rows{kind}"][q]


def places():
    return pl.BlockSpec(memory_space=pl.ANY), pl.BlockSpec(memory_space=pltpu.VMEM)


def scatter(g, dims):
    scratch = Scatter(dims).scratch() | {"unit": pltpu.VMEM((MATS, *UNIT), f32)} | exchange_scratch()
    anywhere, vmem = places()
    rows = [jax.ShapeDtypeStruct((sum(w[0] == kind for w in WAVES), PADS[kind], 4 * C), bf16) for kind, (_, C) in enumerate(SHAPES)]
    *grads, _ = pl.pallas_call(
        functools.partial(scatter_kernel, dims, tuple(scratch)),
        out_shape=(*rows, jax.ShapeDtypeStruct((MATS, *dims, *UNIT), bf16)),
        in_specs=[anywhere],
        out_specs=(vmem, vmem, anywhere),
        scratch_shapes=list(scratch.values()),
        compiler_params=pltpu.CompilerParams(collective_id=1, has_side_effects=True, vmem_limit_bytes=VMEM_MOST),
        name="scatter",
    )(g)
    return grads


class Gather:
    def __init__(self, dims):
        self.colors = [Color(k, dims) for k in range(len(ORDERS))]
        events = [e for c in self.colors for e in c.events(True)]
        timed = []
        for n, (e, character) in enumerate(zip(events, GATHER_TIMES, strict=True)):
            for w in range(MATS):
                timed.append((time_of(character) + GATHER_STEPS[e[2] == START] * w, w, n))
        self.order = [(events[n], w) for _, w, n in sorted(timed)]

    def scratch(self):
        shapes = {}
        for c in self.colors:
            for ring in c.rings:
                for way in ("send", "recv"):
                    shapes[way + ring.name] = pltpu.SemaphoreType.DMA((MATS, ring.n - 1))
        for name in ("over_send", "over_recv"):
            shapes[name] = pltpu.SemaphoreType.DMA((MATS, len(ORDERS)))
        shapes["own"] = pltpu.SemaphoreType.DMA((MATS,))
        return shapes

    def bind(self, torus, out, unit, s):
        self.t, self.out, self.unit, self.s = torus, out, unit, s

    def place(self, c, w, core, **at):
        return self.out.at[(w, *c.index(**at), core, slice(None), c.columns)]

    def own(self, w):
        t = self.t
        return pltpu.make_async_copy(self.unit.at[w], self.out.at[(w, *t.at.values(), t.core)], self.s["own"].at[w])

    def directs(self, ring, w):
        c, t = ring.color, self.t
        src, dst = self.unit.at[w, :, c.columns], self.place(c, w, t.core, **t.at)
        return [direct(t, ring, o, w, src, dst, self.s, w, w) for o in range(1, ring.n)]

    def message(self, ring, side, m, w):
        t, c, s = self.t, ring.color, self.s
        sign = (1 - 2 * side) * (1 - 2 * (w % 2))
        at = {d: t.at[d] for d in c.order[: ring.phase]} | {ring.d: t.wrap(ring.d, t.at[ring.d] - sign * m)}
        block, n = self.place(c, w, t.core, **at), ring.message(side, m)
        return remote(block, block, s["send" + ring.name].at[w, n], s["recv" + ring.name].at[w, n], t.beside(ring.d, sign))

    def over(self, c, w, core, **at):
        block = self.place(c, w, core, **at)
        return remote(block, block, self.s["over_send"].at[w, c.k], self.s["over_recv"].at[w, c.k], self.t.partner())

    def event(self, kind, c, phase, side, j, w):
        ring, t = c.rings[phase], self.t
        if kind == "d":
            for copy in self.directs(ring, w):
                copy.start()
        elif kind == "e":
            for copy in self.directs(ring, w):
                copy.wait_recv()
        elif kind == "s":
            for side in ring.sides:
                self.message(ring, side, 0, w).start()
            if not phase:
                self.over(c, w, t.core, **{ring.d: t.at[ring.d]}).start()
        else:
            self.message(ring, side, j - 1, w).wait_recv()
            if j < ring.steps[side]:
                self.message(ring, side, j, w).start()
            if not phase:
                sign = (1 - 2 * side) * (1 - 2 * (w % 2))
                self.over(c, w, t.core, **{ring.d: t.wrap(ring.d, t.at[ring.d] - sign * j)}).start()

    def finish(self, w):
        for c in self.colors:
            for ring in c.rings:
                if ring.phase == 2:
                    for copy in self.directs(ring, w):
                        copy.wait_send()
                else:
                    for side in ring.sides:
                        for m in range(ring.steps[side]):
                            self.message(ring, side, m, w).wait_send()
            self.over(c, w, self.t.core).wait_send()
            self.over(c, w, 1 - self.t.core).wait_recv()

    def run(self):
        for w in range(MATS):
            self.own(w).wait()
        for e, w in self.order:
            self.event(*e, w)
        for w in range(MATS):
            self.finish(w)


AXES = ("core", "x", "y", "z")


def sum_over_all(t, s, value):
    for n, d in enumerate(AXES):
        mine, box = s["norm_out"].at[n], s["norm_" + d]
        mine[...] = value
        copies = []
        for o in range(box.shape[0]):
            device = t.partner() if d == "core" else t.beside(d, o + 1)
            copies.append(remote(mine, box.at[o], s["norm_send"].at[n, o], s["norm_recv"].at[n, o], device))
        for copy in copies:
            copy.start()
        for copy in copies:
            copy.wait()
        for o in range(box.shape[0]):
            value = value + box[o]
    return value


def update_kernel(dims, names, *refs):
    take = iter(refs)
    grads, w_in, m_in, v_in, m_out, v_out = ([next(take) for _ in range(n)] for n in (2, 3, 3, 3, 3, 3))
    out = next(take)
    s = dict(zip(names, take, strict=True))
    t = Torus(dims)
    t.enter()

    def rows(kind, at):
        return grads[kind][at, 0 : SHAPES[kind][0] // 4, :].astype(f32)

    total, count = jnp.zeros((1, 1), f32), 0
    for kind, at in WAVES:
        g = rows(kind, at)
        count += g.size
        total = total + jnp.sum(jnp.sum(g * g, axis=0, keepdims=True), axis=1, keepdims=True)
    for d in AXES:
        count *= s["norm_" + d].shape[0] + 1
    total = sum_over_all(t, s, jnp.broadcast_to(total, TILE))[0:1, 0:1]
    factor = jnp.minimum(1.0, 0.5 * lax.rsqrt(total / count + 1e-30))

    for kind, at in WAVES:
        which, layer = (2, at) if kind else divmod(at, 2)
        R, C = SHAPES[kind]
        g = rows(kind, at) * factor
        w = w_in[which][layer].astype(f32)
        m = 0.9 * m_in[which][layer] + 0.1 * g
        v = 0.95 * v_in[which][layer] + 0.05 * g * g
        m_out[which][layer] = m
        v_out[which][layer] = v
        w = (w - 0.02 * (m * lax.rsqrt(v + 1e-8) + 0.1 * w)).astype(bf16)
        for q in range(4):
            s[f"slab{kind}"][q, at, 0 : R // 4, :] = w[:, C * q : C * (q + 1)]
    exchange(t, s)
    ga = Gather(dims)
    ga.bind(t, out, s["unit"], s)
    for w, (kind, at) in enumerate(WAVES):
        R, C = SHAPES[kind]
        nat, rows_in, n = s[f"nat{kind}"], s[f"rows{kind}"], R // 4
        for q in range(4):
            nat[q * n : (q + 1) * n, :] = rows_in[q, at, 0:n, :].astype(f32)
        for natural, unit in tiles(R, C):
            s["wide"][unit] = nat[natural]
        s["unit"][w] = s["wide"][...].astype(bf16)
        ga.own(w).start()
    ga.run()


def update(grads, w, m, v, dims):
    scratch = Gather(dims).scratch() | exchange_scratch()
    scratch["unit"] = pltpu.VMEM((MATS, *UNIT), bf16)
    scratch["wide"] = pltpu.VMEM(UNIT, f32)
    scratch["norm_out"] = pltpu.VMEM((len(AXES), *TILE), f32)
    for d, n in zip(AXES, (2, *dims), strict=True):
        scratch["norm_" + d] = pltpu.VMEM((n - 1, *TILE), f32)
    for name in ("norm_send", "norm_recv"):
        scratch[name] = pltpu.SemaphoreType.DMA((len(AXES), max(dims)))
    anywhere, vmem = places()
    given = (*grads, *w, *m, *v)
    like = [jax.ShapeDtypeStruct(a.shape, f32) for a in (*m, *v)]
    *mv, out = pl.pallas_call(
        functools.partial(update_kernel, dims, tuple(scratch)),
        out_shape=(*like, jax.ShapeDtypeStruct((MATS, *dims, 2, *UNIT), bf16)),
        in_specs=[vmem] * len(given),
        out_specs=(*[vmem] * len(like), anywhere),
        scratch_shapes=list(scratch.values()),
        compiler_params=pltpu.CompilerParams(collective_id=2, has_side_effects=True, vmem_limit_bytes=VMEM_SOME),
        name="update",
    )(*given)
    return mv, out


VMEM_MOST, VMEM_SOME = 62 << 20, 40 << 20


def normed(h):
    wide = h.astype(f32)
    scale = lax.rsqrt(jnp.mean(wide**2, -1, keepdims=True) + 1e-6)
    return (wide * scale).astype(bf16)


def dotf(a, b, dims):
    return lax.dot_general(a, b, (dims, ((), ())), preferred_element_type=f32)


def glu(gate, up):
    return jax.nn.silu(gate) * up


def enter_layer(h, wg, wu):
    a, norm_back = jax.vjp(normed, h)
    gate = dotf(a, wg, ((1,), (0,)))
    up = dotf(a, wu, ((1,), (0,)))
    return a, gate, up, lax.optimization_barrier(glu(gate, up).astype(bf16)), norm_back


def back_to_hidden(dh, gate, up, wd):
    dhid = dotf(dh, wd, ((1,), (1,))).astype(bf16).astype(f32)
    dgate, dup = jax.vjp(glu, gate, up)[1](dhid)
    return dgate.astype(bf16), dup.astype(bf16)


def factors(x, dy, wg, wu, wd):
    a0, gate0, up0, hid0, _ = enter_layer(x, wg[0], wu[0])
    h1 = x + dotf(hid0, wd[0], ((1,), (0,))).astype(bf16)
    a1, gate1, up1, hid1, norm_back = enter_layer(h1, wg[1], wu[1])
    dg1, du1 = back_to_hidden(dy, gate1, up1, wd[1])
    da = dotf(dg1, wg[1], ((1,), (1,))).astype(bf16) + dotf(du1, wu[1], ((1,), (1,))).astype(bf16)
    dh1 = dy + norm_back(da)[0]
    dg0, du0 = back_to_hidden(dh1, gate0, up0, wd[0])
    return (hid1, dy), (a1, dg1), (a1, du1), (hid0, dh1), (a0, dg0), (a0, du0)


def product_kernel(kind, left, right, *refs):
    out = refs[-1]
    C, width = SHAPES[kind][1], out.shape[5] * SHAPES[kind][1]
    for start in range(0, width, CHUNK):
        wide = lax.dot_general(left[...], right[:, start : start + CHUNK], (((0,), (0,)), ((), ())), preferred_element_type=f32)
        wide = wide.reshape(out.shape[2], out.shape[3], SHAPES[kind][0], CHUNK)
        if kind:
            for natural, unit in tiles(*DOWN):
                for core in range(out.shape[5]):
                    at = core * C + natural[1].start - start
                    if 0 <= at < CHUNK:
                        out[(0, 0, slice(None), slice(None), 0, core, *unit)] = wide[:, :, natural[0].start : natural[0].start + natural[0].size, at : at + natural[1].size].astype(bf16)
        else:
            for core in range(out.shape[5]):
                begin, end = max(start, core * C), min(start + CHUNK, core * C + C)
                if begin < end:
                    out[0, 0, :, :, 0, core, :, begin - core * C : end - core * C] = wide[..., begin - start : end - start].astype(bf16)


CHUNK = 256


def product(wave, left, right, into, dims):
    X, Y, Z = dims
    kind = WAVES[wave][0]
    R, C = SHAPES[kind]
    tokens, halves = right.shape[0], Z // 2
    given = [] if into is None else [into]
    return pl.pallas_call(
        functools.partial(product_kernel, kind),
        grid=(2, X),
        out_shape=jax.ShapeDtypeStruct((MATS, X, Y, halves, 2, 2, *UNIT), bf16),
        in_specs=[pl.BlockSpec((tokens, R * Y * halves), lambda p, i: (0, i)), pl.BlockSpec((tokens, 2 * C), lambda p, i: (0, p))]
        + [pl.BlockSpec(memory_space=pl.ANY)] * len(given),
        out_specs=pl.BlockSpec((1, 1, Y, halves, 1, 2, *UNIT), lambda p, i: (wave, i, 0, 0, p, 0, 0, 0)),
        input_output_aliases={2: 0} if given else {},
        cost_estimate=pl.CostEstimate(flops=2 * left.size * right.shape[1], bytes_accessed=2 * left.shape[1] * right.shape[1], transcendentals=0),
        compiler_params=pltpu.CompilerParams(vmem_limit_bytes=VMEM_SOME),
        name="product",
    )(left, right, *given)


def settle_kernel(kind, w, out):
    R, C = SHAPES[kind]
    for p in range(2):
        for core in range(2):
            q = 2 * p + core
            block = w.at[0, 0, :, :, p, core]
            if kind:
                for natural, unit in tiles(*DOWN):
                    out[:, :, :, natural[0], pl.ds(C * q + natural[1].start, natural[1].size)] = block[(slice(None), slice(None), *unit)][None]
            else:
                out[:, :, :, :, C * q : C * (q + 1)] = block[...][None]


def settle(w, waves, dims):
    X, Y, Z = dims
    kind = WAVES[waves[0]][0]
    R, C = SHAPES[kind]
    halves = Z // 2
    out = pl.pallas_call(
        functools.partial(settle_kernel, kind),
        grid=(2, X),
        out_shape=jax.ShapeDtypeStruct((2, X * Y, halves, R, 4 * C), bf16),
        in_specs=[pl.BlockSpec((1, 1, Y, halves, 2, 2, *UNIT), lambda n, i: (waves[0] + (waves[1] - waves[0]) * n, i, 0, 0, 0, 0, 0, 0))],
        out_specs=pl.BlockSpec((1, Y, halves, R, 4 * C), lambda n, i: (n, i, 0, 0, 0)),
        compiler_params=pltpu.CompilerParams(vmem_limit_bytes=VMEM_SOME),
        name="settle",
    )(w)
    return out.reshape(2, -1, 4 * C)


def device_step(dims, x, dy, wg, wu, wd, *moments):
    X, Y, Z = dims
    m, v = moments[:3], moments[3:]
    g = None
    for wave, (left, right) in enumerate(factors(x[0], dy[0], wg, wu, wd)):
        g = product(wave, left, right, g, dims)
    grads = scatter(g.reshape(MATS, *dims, 2, *UNIT), dims)
    place = lax.axis_index("dp")
    w = [lax.dynamic_slice_in_dim(a, place * b.shape[1], b.shape[1], 1) for a, b in zip((wg, wu, wd), m, strict=True)]
    mv, out = update(grads, w, m, v, dims)
    out = out.reshape(MATS, X, Y, Z // 2, 2, 2, *UNIT)
    waves = [[WAVES.index((1, n) if which == 2 else (0, 2 * which + n)) for n in range(2)] for which in range(3)]
    return (*[settle(out, pair, dims) for pair in waves], *mv)


DIMS = {256: (4, 4, 8)}


def solution(mesh):
    dims = DIMS[mesh.shape["dp"]]
    spec = jax.sharding.PartitionSpec
    tokens, whole, rows = spec(("rep", "dp")), spec(), spec(None, "dp", None)
    return jax.shard_map(
        functools.partial(device_step, dims),
        mesh=mesh,
        in_specs=(tokens, tokens, *[whole] * 3, *[rows] * 6),
        out_specs=(*[spec("rep")] * 3, *[spec("rep", "dp", None)] * 6),
        check_vma=False,
    )
```

profile of v0, /device:TPU:1, one launch (start us, length us, event | category | flops | bytes accessed | tf_op | source)
XLA Modules:
  0.0 714.4 jit_solution(16220247698242192814)
XLA Ops:
  0.6 2.6 fusion.43
  3.2 2.5 fusion.44.left
  5.7 18.4 %fusion.26 = f32[1024,3584]{1,0:T(8,128)} fusion(bf16[2,1536,3584]{2,1,0:T(8,128)(2,1)} %param.13, bf16[1,1024,1536]{2,1,0:T(8,128)(2,1)} %param.11, f32[1024]{0:T(1024)S(1)} %add_rsqrt_fusion), kind=kOutput, calls=%fused_computation.36 | convolution fusion | flops 11279007744 | bytes 28839936 | tf_op jit(solution)/shard_map/dot_general | solution.py:582
  24.1 22.3 %multiply_convert_fusion.1 = (bf16[1024,3584]{1,0:T(8,128)(2,1)}, f32[1024,3584]{1,0:T(8,128)}) fusion(f32[1024,3584]{1,0:T(8,128)} %fusion.26, bf16[2,1536,3584]{2,1,0:T(8,128)(2,1)} %param.14, bf16[1,1024,1536]{2,1,0:T(8,128)(2,1)} %param.11, f32[1024]{0:T(1024)S(1)} %add_rsqrt_fusion), kind=kOutput, calls=%fused_computation.17 | convolution fusion | flops 11301027840 | bytes 50860032 | tf_op jit(solution)/shard_map/dot_general | solution.py:582
  46.4 16.8 %fusion.47 = (f32[1024]{0:T(1024)S(1)}, bf16[1024,1536]{1,0:T(8,128)(2,1)S(1)}) fusion(bf16[1024,3584]{1,0:T(8,128)(2,1)} %get-tuple-element.41.left, bf16[2,3584,1536]{2,1,0:T(8,128)(2,1)} %param.15, bf16[1,1024,1536]{2,1,0:T(8,128)(2,1)} %param.11), kind=kOutput, calls=%fused_computation.60 | convolution fusion | flops 11282152448 | bytes 24645632 | tf_op jit(solution)/shard_map/dot_general | solution.py:582
  63.8 18.0 %fusion.12 = f32[1024,3584]{1,0:T(8,128)} fusion(bf16[1024,1536]{1,0:T(8,128)(2,1)S(1)} %fusion.48.left, bf16[2,1536,3584]{2,1,0:T(8,128)(2,1)} %param.13), kind=kOutput, calls=%fused_computation.22 | convolution fusion | flops 11274289152 | bytes 28835840 | tf_op jit(solution)/shard_map/dot_general | solution.py:582
  81.8 16.2 %fusion.37 = bf16[1024,3584]{1,0:T(8,128)(2,1)} fusion(bf16[2,3584,1536]{2,1,0:T(8,128)(2,1)} %param.15, bf16[1,1024,1536]{2,1,0:T(8,128)(2,1)S(1)} %copy-done), kind=kOutput, calls=%fused_computation.54 | convolution fusion | flops 11277959168 | bytes 21495808 | tf_op jit(solution)/shard_map/dot_general | solution.py:582
  98.0 27.4 %multiply_convert_fusion = (bf16[1024,3584]{1,0:T(8,128)(2,1)}, bf16[1024,3584]{1,0:T(8,128)(2,1)}, bf16[1024,3584]{1,0:T(8,128)(2,1)}) fusion(f32[1024,3584]{1,0:T(8,128)} %fusion.12, bf16[1024,3584]{1,0:T(8,128)(2,1)} %fusion.37, bf16[1024,1536]{1,0:T(8,128)(2,1)S(1)} %fusion.48.left, bf16[2,1536,3584]{2,1,0:T(8,128)(2,1)} %param.14), kind=kOutput, calls=%fused_computation.14 | convolution fusion | flops 11336679424 | bytes 58195968 | tf_op jit(solution)/shard_map/dot_general | solution.py:582
  125.4 17.3 %fusion.53 = bf16[1024,1536]{1,0:T(8,128)(2,1)} fusion(bf16[1024,3584]{1,0:T(8,128)(2,1)} %get-tuple-element.38.right, bf16[2,1536,3584]{2,1,0:T(8,128)(2,1)} %param.14), kind=kOutput, calls=%fused_computation.65 | convolution fusion | flops 11275862016 | bytes 21495808 | tf_op jit(solution)/shard_map/dot_general | solution.py:582
  142.7 18.0 %fusion.49 = (f32[1024]{0:T(1024)S(1)}, bf16[1024,1536]{1,0:T(8,128)(2,1)}) fusion(bf16[1024,1536]{1,0:T(8,128)(2,1)S(1)} %get-tuple-element.44, bf16[1024,1536]{1,0:T(8,128)(2,1)} %fusion.53, bf16[1024,3584]{1,0:T(8,128)(2,1)} %get-tuple-element.37.right, bf16[2,1536,3584]{2,1,0:T(8,128)(2,1)} %param.13), kind=kOutput, calls=%fused_computation.62 | convolution fusion | flops 11283725312 | bytes 27791360 | tf_op jit(solution)/shard_map/dot_general | solution.py:582
  160.6 3.2 fusion.66.right
  163.8 26.1 %fusion.7 = (bf16[1024,3584]{1,0:T(8,128)(2,1)}, bf16[1024,3584]{1,0:T(8,128)(2,1)}) fusion(f32[1024,3584]{1,0:T(8,128)} %fusion.26, f32[1024,3584]{1,0:T(8,128)} %get-tuple-element.42, bf16[1024,1536]{1,0:T(8,128)(2,1)S(1)} %fusion.66.right, bf16[2,3584,1536]{2,1,0:T(8,128)(2,1)} %param.15), kind=kOutput, calls=%fused_computation.13 | convolution fusion | flops 11333009408 | bytes 58195968 | tf_op jit(solution)/shard_map/dot_general | solution.py:582
  189.9 3.1 copy-done.1
  193.0 15.9 %product.6.refs_0_ = bf16[6,4,4,4,2,2,24,896]{7,6,5,4,3,2,1,0:T(8,128)(2,1)} custom-call(bf16[1024,3584]{1,0:T(8,128)(2,1)S(1)} %copy-done.1, bf16[1024,1536]{1,0:T(8,128)(2,1)S(1)} %bitcast.73), custom_call_target="tpu_custom_call" | custom-call | flops 11274289152 | bytes 11010048 | tf_op jit(solution)/shard_map/product/pallas_call | solution.py:641
  208.8 3.1 copy-done.4
  211.9 15.8 %product.7.refs_0_ = bf16[6,4,4,4,2,2,24,896]{7,6,5,4,3,2,1,0:T(8,128)(2,1)} custom-call(bf16[1024,1536]{1,0:T(8,128)(2,1)S(1)} %fusion.48.left, bf16[1024,3584]{1,0:T(8,128)(2,1)S(1)} %copy-done.4, bf16[6,4,4,4,2,2,24,896]{7,6,5,4,3,2,1,0:T(8,128)(2,1)} %product.6.refs_0_), custom_call_target="tpu_custom_call", output_to_operand_aliasing={{}: (2, {})} | custom-call | flops 11274289152 | bytes 11010048 | tf_op jit(solution)/shard_map/product/pallas_call | solution.py:641
  227.8 3.1 copy-done.3
  230.8 15.6 %product.8.refs_0_ = bf16[6,4,4,4,2,2,24,896]{7,6,5,4,3,2,1,0:T(8,128)(2,1)} custom-call(bf16[1024,1536]{1,0:T(8,128)(2,1)S(1)} %fusion.48.left, bf16[1024,3584]{1,0:T(8,128)(2,1)S(1)} %copy-done.3, bf16[6,4,4,4,2,2,24,896]{7,6,5,4,3,2,1,0:T(8,128)(2,1)} %product.7.refs_0_), custom_call_target="tpu_custom_call", output_to_operand_aliasing={{}: (2, {})} | custom-call | flops 11274289152 | bytes 11010048 | tf_op jit(solution)/shard_map/product/pallas_call | solution.py:641
  246.4 3.1 copy-done.2
  249.5 15.9 %product.9.refs_0_ = bf16[6,4,4,4,2,2,24,896]{7,6,5,4,3,2,1,0:T(8,128)(2,1)} custom-call(bf16[1024,3584]{1,0:T(8,128)(2,1)S(1)} %copy-done.2, bf16[1024,1536]{1,0:T(8,128)(2,1)S(1)} %fusion.66.right, bf16[6,4,4,4,2,2,24,896]{7,6,5,4,3,2,1,0:T(8,128)(2,1)} %product.8.refs_0_), custom_call_target="tpu_custom_call", output_to_operand_aliasing={{}: (2, {})} | custom-call | flops 11274289152 | bytes 11010048 | tf_op jit(solution)/shard_map/product/pallas_call | solution.py:641
  265.4 3.1 copy-done.5
  268.5 15.6 %product.10.refs_0_ = bf16[6,4,4,4,2,2,24,896]{7,6,5,4,3,2,1,0:T(8,128)(2,1)} custom-call(bf16[1024,1536]{1,0:T(8,128)(2,1)S(1)} %fusion.44.left, bf16[1024,3584]{1,0:T(8,128)(2,1)S(1)} %copy-done.5, bf16[6,4,4,4,2,2,24,896]{7,6,5,4,3,2,1,0:T(8,128)(2,1)} %product.9.refs_0_), custom_call_target="tpu_custom_call", output_to_operand_aliasing={{}: (2, {})} | custom-call | flops 11274289152 | bytes 11010048 | tf_op jit(solution)/shard_map/product/pallas_call | solution.py:641
  284.1 15.6 %product.11 = bf16[6,4,4,4,2,2,24,896]{7,6,5,4,3,2,1,0:T(8,128)(2,1)} custom-call(bf16[1024,1536]{1,0:T(8,128)(2,1)S(1)} %fusion.44.left, bf16[1024,3584]{1,0:T(8,128)(2,1)S(1)} %bitcast.75, bf16[6,4,4,4,2,2,24,896]{7,6,5,4,3,2,1,0:T(8,128)(2,1)} %product.10.refs_0_), custom_call_target="tpu_custom_call", output_to_operand_aliasing={{}: (2, {})} | custom-call | flops 11274289152 | bytes 11010048 | tf_op jit(solution)/shard_map/product/pallas_call | solution.py:641
  299.7 185.0 %scatter.1 = (bf16[4,8,3584]{2,1,0:T(8,128)(2,1)}, bf16[2,16,1536]{2,1,0:T(8,128)(2,1)}, bf16[6,4,4,8,24,896]{5,4,3,2,1,0:T(8,128)(2,1)}) custom-call(bf16[6,4,4,8,2,24,896]{6,5,4,3,2,1,0:T(8,128)(2,1)} %bitcast.76), custom_call_target="tpu_custom_call" | custom-call | tf_op jit(solution)/shard_map/scatter/pallas_call | solution.py:378
  484.8 1.1 constant_dynamic-slice_fusion.1
  485.9 1.0 constant_dynamic-slice_fusion.refs_4_
  487.2 0.9 copy-done.6
  488.2 0.9 copy-done.7
  489.1 169.5 %update.1 = (f32[2,6,3584]{2,1,0:T(8,128)S(1)}, f32[2,6,3584]{2,1,0:T(8,128)S(1)}, f32[2,14,1536]{2,1,0:T(8,128)S(1)}, f32[2,6,3584]{2,1,0:T(8,128)S(1)}, f32[2,...) custom-call(bf16[4,8,3584]{2,1,0:T(8,128)(2,1)S(1)} %copy-done.6, ...), custom_call_target="tpu_custom_call" | custom-call | tf_op jit(solution)/shard_map/update/pallas_call | solution.py:560
  658.6 16.8 %settle.3 = bf16[2,16,4,24,3584]{4,3,2,1,0:T(8,128)(2,1)} custom-call(bf16[6,4,4,4,2,2,24,896]{7,6,5,4,3,2,1,0:T(8,128)(2,1)} %bitcast.77), custom_call_target="tpu_custom_call" | custom-call | tf_op jit(solution)/shard_map/settle/pallas_call | solution.py:673
  675.4 16.8 %settle.4 = bf16[2,16,4,24,3584]{4,3,2,1,0:T(8,128)(2,1)} custom-call(bf16[6,4,4,4,2,2,24,896]{7,6,5,4,3,2,1,0:T(8,128)(2,1)} %bitcast.78), custom_call_target="tpu_custom_call" | custom-call | tf_op jit(solution)/shard_map/settle/pallas_call | solution.py:673
  692.2 17.0 %settle.5 = bf16[2,16,4,56,1536]{4,3,2,1,0:T(8,128)(2,1)} custom-call(bf16[6,4,4,4,2,2,24,896]{7,6,5,4,3,2,1,0:T(8,128)(2,1)} %bitcast.79), custom_call_target="tpu_custom_call" | custom-call | tf_op jit(solution)/shard_map/settle/pallas_call | solution.py:673
  (42 shorter events, 5.7 us)
Async XLA Ops:
  63.8 18.0 %copy-start = (bf16[1,1024,1536]{2,1,0:T(8,128)(2,1)S(1)}, bf16[1,1024,1536]{2,1,0:T(8,128)(2,1)}, u32[]{:S(2)}) copy-start(bf16[1,1024,1536]{2,1,0:T(8,128)(2,1)} %param.12) | copy-start | bytes 9437188
  189.9 3.1 copy-start.1
  208.8 3.1 copy-start.4
  227.8 3.1 copy-start.3
  246.4 3.1 copy-start.2
  249.5 34.6 %slice-start = ((s8[7340032]{0:T(1024)(128)(4,1)}), s8[3145728]{0:T(1024)(128)(4,1)S(1)}, s32[]{:S(2)}) async-start(s8[7340032]{0:T(1024)(128)(4,1)} %bitcast.74), calls=%async_computation | async-start | bytes 6291456
  265.4 3.1 copy-start.5
  268.5 15.6 %slice-start.1 = ((s8[7340032]{0:T(1024)(128)(4,1)}), s8[4194304]{0:T(1024)(128)(4,1)S(1)}, s32[]{:S(2)}) async-start(s8[7340032]{0:T(1024)(128)(4,1)} %bitcast.74), calls=%async_computation.1 | async-start | bytes 8388608
  299.7 187.2 %copy-start.8 = (f32[2,6,3584]{2,0,1:T(2,128)S(1)}, f32[2,6,3584]{2,0,1:T(2,128)}, u32[]{:S(2)}) copy-start(f32[2,6,3584]{2,0,1:T(2,128)} %param.16) | copy-start | bytes 516100
  299.7 187.2 %copy-start.9 = (f32[2,6,3584]{2,0,1:T(2,128)S(1)}, f32[2,6,3584]{2,0,1:T(2,128)}, u32[]{:S(2)}) copy-start(f32[2,6,3584]{2,0,1:T(2,128)} %param.17) | copy-start | bytes 516100
  299.7 187.3 %copy-start.10 = (f32[2,14,1536]{2,0,1:T(2,128)S(1)}, f32[2,14,1536]{2,0,1:T(2,128)}, u32[]{:S(2)}) copy-start(f32[2,14,1536]{2,0,1:T(2,128)} %param.18) | copy-start | bytes 516100
  299.7 187.4 %copy-start.11 = (f32[2,6,3584]{2,0,1:T(2,128)S(1)}, f32[2,6,3584]{2,0,1:T(2,128)}, u32[]{:S(2)}) copy-start(f32[2,6,3584]{2,0,1:T(2,128)} %param.19) | copy-start | bytes 516100
  299.7 187.4 %copy-start.12 = (f32[2,6,3584]{2,0,1:T(2,128)S(1)}, f32[2,6,3584]{2,0,1:T(2,128)}, u32[]{:S(2)}) copy-start(f32[2,6,3584]{2,0,1:T(2,128)} %param.20) | copy-start | bytes 516100
  299.7 187.5 %copy-start.13 = (f32[2,14,1536]{2,0,1:T(2,128)S(1)}, f32[2,14,1536]{2,0,1:T(2,128)}, u32[]{:S(2)}) copy-start(f32[2,14,1536]{2,0,1:T(2,128)} %param.21) | copy-start | bytes 516100
  487.2 0.9 copy-start.6
  488.2 0.9 copy-start.7
where the time goes:
time: 723 us; the launch traced here: 714 us
  Pallas kernels  499 us (69%)
  matrix products  180 us (25%)
  local copies, waits for them, and re-layouts  24.4 us (3%)
  other arithmetic  8.79 us (1%)
    pallas_call x1, Pallas kernels, scatter(): pl.pallas_call(functools.partial(scatter_kernel, dims, tuple(scratch)), o...  185 us
    dot_general x9, matrix products, dotf(): return lax.dot_general(a, b, (dims, ((), ())), preferred_element_type=f32)  180 us
    pallas_call x1, Pallas kernels, update(): pl.pallas_call(functools.partial(update_kernel, dims, tuple(scratch)), ou...  170 us
    pallas_call x6, Pallas kernels, product(): pl.pallas_call(functools.partial(product_kernel, kind), grid=(2, X), out_...  94.4 us
    pallas_call x3, Pallas kernels, settle(): pl.pallas_call(functools.partial(settle_kernel, kind), grid=(2, X), out_s...  50.5 us
    unnamed x44, local copies, waits for them, and re-layouts  22.4 us

commit v1 on v0

--- a/solution.py
+++ b/solution.py
@@ -412,11 +412,11 @@
         self.t, self.out, self.unit, self.s = torus, out, unit, s
 
     def place(self, c, w, core, **at):
-        return self.out.at[(w, *c.index(**at), core, slice(None), c.columns)]
+        return self.out[w].at[(*c.index(**at), core, slice(None), c.columns)]
 
     def own(self, w):
         t = self.t
-        return pltpu.make_async_copy(self.unit.at[w], self.out.at[(w, *t.at.values(), t.core)], self.s["own"].at[w])
+        return pltpu.make_async_copy(self.unit.at[w], self.out[w].at[(*t.at.values(), t.core)], self.s["own"].at[w])
 
     def directs(self, ring, w):
         c, t = ring.color, self.t
@@ -500,7 +500,7 @@
 def update_kernel(dims, names, *refs):
     take = iter(refs)
     grads, w_in, m_in, v_in, m_out, v_out = ([next(take) for _ in range(n)] for n in (2, 3, 3, 3, 3, 3))
-    out = next(take)
+    out = [next(take) for _ in WAVES]
     s = dict(zip(names, take, strict=True))
     t = Torus(dims)
     t.enter()
@@ -523,10 +523,10 @@
         R, C = SHAPES[kind]
         g = rows(kind, at) * factor
         w = w_in[which][layer].astype(f32)
-        m = 0.9 * m_in[which][layer] + 0.1 * g
-        v = 0.95 * v_in[which][layer] + 0.05 * g * g
-        m_out[which][layer] = m
-        v_out[which][layer] = v
+        m = 0.9 * m_in[which][:, layer, :] + 0.1 * g
+        v = 0.95 * v_in[which][:, layer, :] + 0.05 * g * g
+        m_out[which][:, layer, :] = m
+        v_out[which][:, layer, :] = v
         w = (w - 0.02 * (m * lax.rsqrt(v + 1e-8) + 0.1 * w)).astype(bf16)
         for q in range(4):
             s[f"slab{kind}"][q, at, 0 : R // 4, :] = w[:, C * q : C * (q + 1)]
@@ -545,7 +545,14 @@
     ga.run()
 
 
-def update(grads, w, m, v, dims):
+IN_VMEM = (1, 2, 4)
+
+
+def home(wave):
+    return pltpu.VMEM if wave in IN_VMEM else pltpu.HBM
+
+
+def update(grads, w, moments, dims):
     scratch = Gather(dims).scratch() | exchange_scratch()
     scratch["unit"] = pltpu.VMEM((MATS, *UNIT), bf16)
     scratch["wide"] = pltpu.VMEM(UNIT, f32)
@@ -555,21 +562,22 @@
     for name in ("norm_send", "norm_recv"):
         scratch[name] = pltpu.SemaphoreType.DMA((len(AXES), max(dims)))
     anywhere, vmem = places()
-    given = (*grads, *w, *m, *v)
-    like = [jax.ShapeDtypeStruct(a.shape, f32) for a in (*m, *v)]
-    *mv, out = pl.pallas_call(
+    given = (*grads, *w, *moments)
+    like = [jax.ShapeDtypeStruct(a.shape, f32) for a in moments]
+    results = pl.pallas_call(
         functools.partial(update_kernel, dims, tuple(scratch)),
-        out_shape=(*like, jax.ShapeDtypeStruct((MATS, *dims, 2, *UNIT), bf16)),
+        out_shape=like + [home(w)((*dims, 2, *UNIT), bf16) for w in range(MATS)],
         in_specs=[vmem] * len(given),
-        out_specs=(*[vmem] * len(like), anywhere),
+        out_specs=[vmem] * len(like) + [anywhere] * MATS,
         scratch_shapes=list(scratch.values()),
-        compiler_params=pltpu.CompilerParams(collective_id=2, has_side_effects=True, vmem_limit_bytes=VMEM_SOME),
+        compiler_params=pltpu.CompilerParams(collective_id=2, has_side_effects=True, vmem_limit_bytes=VMEM_FEW),
         name="update",
     )(*given)
-    return mv, out
-
-
-VMEM_MOST, VMEM_SOME = 62 << 20, 40 << 20
+    return results[: len(like)], results[len(like) :]
+
+
+VMEM_MOST, VMEM_SOME, VMEM_FEW = 62 << 20, 40 << 20, 12 << 20
+VMEM_HALF = 20 << 20
 
 
 def normed(h):
@@ -578,36 +586,144 @@
     return (wide * scale).astype(bf16)
 
 
-def dotf(a, b, dims):
+def norm_back(h, da):
+    wide, da = h.astype(f32), da.astype(f32)
+    scale = lax.rsqrt(jnp.mean(wide**2, -1, keepdims=True) + 1e-6)
+    inner = jnp.mean(wide * da, -1, keepdims=True)
+    return (scale * da - wide * (inner * scale * scale * scale)).astype(bf16)
+
+
+PLAIN, TURNED = ((1,), (0,)), ((1,), (1,))
+ROWS = 128
+
+
+def dot(a, b, dims):
     return lax.dot_general(a, b, (dims, ((), ())), preferred_element_type=f32)
 
 
-def glu(gate, up):
-    return jax.nn.silu(gate) * up
-
-
-def enter_layer(h, wg, wu):
-    a, norm_back = jax.vjp(normed, h)
-    gate = dotf(a, wg, ((1,), (0,)))
-    up = dotf(a, wu, ((1,), (0,)))
-    return a, gate, up, lax.optimization_barrier(glu(gate, up).astype(bf16)), norm_back
-
-
-def back_to_hidden(dh, gate, up, wd):
-    dhid = dotf(dh, wd, ((1,), (1,))).astype(bf16).astype(f32)
-    dgate, dup = jax.vjp(glu, gate, up)[1](dhid)
-    return dgate.astype(bf16), dup.astype(bf16)
+def by_rows(ref, work):
+    def some(i, _):
+        work(pl.ds(pl.multiple_of(i * ROWS, ROWS), ROWS))
+        return 0
+
+    lax.fori_loop(0, ref.shape[0] // ROWS, some, 0)
+
+
+def gate_back(dhid, gate, up):
+    soft = jax.nn.sigmoid(gate)
+    return dhid * up * (soft * (1.0 + gate * (1.0 - soft))), dhid * (gate * soft)
+
+
+def bottom_kernel(h, wg, wu, wd, a, gate, up, hid, out, acc):
+    step = pl.program_id(0)
+
+    @pl.when(step == 0)
+    def _():
+        def first(rows):
+            a[rows] = normed(h[rows])
+
+        by_rows(h, first)
+
+    for part in parts():
+        gate[:, part] = dot(a[...], wg[0, :, part], PLAIN)
+        up[:, part] = dot(a[...], wu[0, :, part], PLAIN)
+        hid[:, part] = (jax.nn.silu(gate[:, part]) * up[:, part]).astype(bf16)
+    term = dot(hid[...], wd[0], PLAIN)
+
+    @pl.when(step == 0)
+    def _():
+        acc[...] = term
+
+    @pl.when(step > 0)
+    def _():
+        acc[...] += term
+
+    @pl.when(step == pl.num_programs(0) - 1)
+    def _():
+        def last(rows):
+            out[rows] = h[rows] + acc[rows].astype(bf16)
+
+        by_rows(h, last)
+
+
+def top_kernel(h, dy, wg, wu, wd, a, hid, dgate, dup, dh, acc_gate, acc_up):
+    step = pl.program_id(0)
+
+    @pl.when(step == 0)
+    def _():
+        def first(rows):
+            a[rows] = normed(h[rows])
+
+        by_rows(h, first)
+
+    for part in parts():
+        gate = dot(a[...], wg[0, :, part], PLAIN)
+        up = dot(a[...], wu[0, :, part], PLAIN)
+        dhid = dot(dy[...], wd[0, part, :], TURNED).astype(bf16).astype(f32)
+        hid[:, part] = (jax.nn.silu(gate) * up).astype(bf16)
+        by_gate, by_up = gate_back(dhid, gate, up)
+        dgate[:, part], dup[:, part] = by_gate.astype(bf16), by_up.astype(bf16)
+    for acc, d, w in ((acc_gate, dgate, wg), (acc_up, dup, wu)):
+        term = dot(d[...], w[0], TURNED)
+
+        @pl.when(step == 0)
+        def _():
+            acc[...] = term
+
+        @pl.when(step > 0)
+        def _():
+            acc[...] += term
+
+    @pl.when(step == pl.num_programs(0) - 1)
+    def _():
+        def last(rows):
+            da = acc_gate[rows].astype(bf16) + acc_up[rows].astype(bf16)
+            dh[rows] = dy[rows] + norm_back(h[rows], da)
+
+        by_rows(h, last)
+
+
+def back_kernel(dh, gate, up, wd, dgate, dup):
+    for part in parts():
+        dhid = dot(dh[...], wd[0, part, :], TURNED).astype(bf16).astype(f32)
+        by_gate, by_up = gate_back(dhid, gate[:, part], up[:, part])
+        dgate[:, part], dup[:, part] = by_gate.astype(bf16), by_up.astype(bf16)
+
+
+WIDTH, PART = 512, 256
+
+
+def parts():
+    return [slice(at, at + PART) for at in range(0, WIDTH, PART)]
+
+
+def layer_call(kernel, layer, tokens_in, hidden_in, weights, hidden_out, tokens_out, accumulators, products, name):
+    T, D = tokens_in[0].shape
+    FF = weights[-1].shape[1]
+    whole = pl.BlockSpec((T, D), lambda n: (0, 0))
+    part = pl.BlockSpec((T, WIDTH), lambda n: (0, n))
+    specs = [pl.BlockSpec((1, D, WIDTH), lambda n: (layer, 0, n))] * (len(weights) - 1) + [pl.BlockSpec((1, WIDTH, D), lambda n: (layer, n, 0))]
+    early, late = tokens_out
+    shape = jax.ShapeDtypeStruct
+    return pl.pallas_call(
+        kernel,
+        grid=(FF // WIDTH,),
+        in_specs=[whole] * len(tokens_in) + [part] * len(hidden_in) + specs,
+        out_specs=[whole] * early + [part] * len(hidden_out) + [whole] * late,
+        out_shape=[shape((T, D), bf16)] * early + [shape((T, FF), t) for t in hidden_out] + [shape((T, D), bf16)] * late,
+        scratch_shapes=[pltpu.VMEM((T, D), f32)] * accumulators,
+        cost_estimate=pl.CostEstimate(flops=2 * products * T * D * FF, bytes_accessed=2 * len(weights) * D * FF, transcendentals=T * FF),
+        compiler_params=pltpu.CompilerParams(vmem_limit_bytes=VMEM_MOST),
+        name=name,
+    )(*tokens_in, *hidden_in, *weights)
 
 
 def factors(x, dy, wg, wu, wd):
-    a0, gate0, up0, hid0, _ = enter_layer(x, wg[0], wu[0])
-    h1 = x + dotf(hid0, wd[0], ((1,), (0,))).astype(bf16)
-    a1, gate1, up1, hid1, norm_back = enter_layer(h1, wg[1], wu[1])
-    dg1, du1 = back_to_hidden(dy, gate1, up1, wd[1])
-    da = dotf(dg1, wg[1], ((1,), (1,))).astype(bf16) + dotf(du1, wu[1], ((1,), (1,))).astype(bf16)
-    dh1 = dy + norm_back(da)[0]
-    dg0, du0 = back_to_hidden(dh1, gate0, up0, wd[0])
-    return (hid1, dy), (a1, dg1), (a1, du1), (hid0, dh1), (a0, dg0), (a0, du0)
+    weights = (wg, wu, wd)
+    a0, gate, up, hid0, h = layer_call(bottom_kernel, 0, (x,), (), weights, (f32, f32, bf16), (1, 1), 1, 3, "bottom")
+    a1, hid1, dg1, du1, dh = layer_call(top_kernel, 1, (h, dy), (), weights, (bf16,) * 3, (1, 1), 2, 5, "top")
+    dg0, du0 = layer_call(back_kernel, 0, (dh,), (gate, up), (wd,), (bf16,) * 2, (0, 0), 0, 1, "back")
+    return (hid1, dy), (a1, dg1), (a1, du1), (hid0, dh), (a0, dg0), (a0, du0)
 
 
 def product_kernel(kind, left, right, *refs):
@@ -647,43 +763,65 @@
         out_specs=pl.BlockSpec((1, 1, Y, halves, 1, 2, *UNIT), lambda p, i: (wave, i, 0, 0, p, 0, 0, 0)),
         input_output_aliases={2: 0} if given else {},
         cost_estimate=pl.CostEstimate(flops=2 * left.size * right.shape[1], bytes_accessed=2 * left.shape[1] * right.shape[1], transcendentals=0),
-        compiler_params=pltpu.CompilerParams(vmem_limit_bytes=VMEM_SOME),
+        compiler_params=pltpu.CompilerParams(vmem_limit_bytes=VMEM_MOST),
         name="product",
     )(left, right, *given)
 
 
-def settle_kernel(kind, w, out):
-    R, C = SHAPES[kind]
-    for p in range(2):
-        for core in range(2):
-            q = 2 * p + core
-            block = w.at[0, 0, :, :, p, core]
-            if kind:
-                for natural, unit in tiles(*DOWN):
-                    out[:, :, :, natural[0], pl.ds(C * q + natural[1].start, natural[1].size)] = block[(slice(None), slice(None), *unit)][None]
-            else:
-                out[:, :, :, :, C * q : C * (q + 1)] = block[...][None]
-
-
-def settle(w, waves, dims):
+SETTLED = (4, 1, 5, 2, 3, 0)
+SHARE = 2
+
+
+def settle_kernel(*refs):
+    step = pl.program_id(0)
+    for n, (wave, w) in enumerate(zip(SETTLED, refs)):
+        kind, out = WAVES[wave][0], refs[MATS + n // 2]
+        C = SHAPES[kind][1]
+
+        @pl.when(step == n)
+        def _():
+            for q in range(4):
+                block = w.at[0, :, :, q // 2, q % 2]
+                if kind:
+                    for natural, unit in tiles(*DOWN):
+                        out[:, :, :, natural[0], pl.ds(C * q + natural[1].start, natural[1].size)] = block[(slice(None), slice(None), *unit)][None]
+                else:
+                    out[:, :, :, :, C * q : C * (q + 1)] = block[...][None]
+
+
+def settle(waves, dims):
     X, Y, Z = dims
-    kind = WAVES[waves[0]][0]
-    R, C = SHAPES[kind]
-    halves = Z // 2
-    out = pl.pallas_call(
-        functools.partial(settle_kernel, kind),
-        grid=(2, X),
-        out_shape=jax.ShapeDtypeStruct((2, X * Y, halves, R, 4 * C), bf16),
-        in_specs=[pl.BlockSpec((1, 1, Y, halves, 2, 2, *UNIT), lambda n, i: (waves[0] + (waves[1] - waves[0]) * n, i, 0, 0, 0, 0, 0, 0))],
-        out_specs=pl.BlockSpec((1, Y, halves, R, 4 * C), lambda n, i: (n, i, 0, 0, 0)),
-        compiler_params=pltpu.CompilerParams(vmem_limit_bytes=VMEM_SOME),
+    X, Y, halves = X * SHARE, Y // SHARE, Z // 2
+    shape = (Y, halves, 2, 2, *UNIT)
+
+    def turn(first, last, n, i):
+        return jnp.clip((n - first) * X + i, 0, (last - first + 1) * X - 1)
+
+    def given(n):
+        return pl.BlockSpec((1, *shape), lambda k, i: (turn(n, n, k, i), *[0] * len(shape)))
+
+    def made(which):
+        R, C = SHAPES[which // 2]
+
+        def place(k, i):
+            at = turn(2 * which, 2 * which + 1, k, i)
+            return (at // X, at % X, 0, 0, 0)
+
+        return pl.BlockSpec((1, Y, halves, R, 4 * C), place)
+
+    outs = pl.pallas_call(
+        settle_kernel,
+        grid=(MATS, X),
+        out_shape=[jax.ShapeDtypeStruct((2, X * Y, halves, SHAPES[which // 2][0], 4 * SHAPES[which // 2][1]), bf16) for which in range(3)],
+        in_specs=[given(n) for n in range(MATS)],
+        out_specs=[made(which) for which in range(3)],
+        compiler_params=pltpu.CompilerParams(vmem_limit_bytes=VMEM_HALF),
         name="settle",
-    )(w)
-    return out.reshape(2, -1, 4 * C)
+    )(*[pltpu.with_memory_space_constraint(waves[n].reshape(X, *shape), home(n)) for n in SETTLED])
+    return [out.reshape(2, -1, out.shape[-1]) for out in outs]
 
 
 def device_step(dims, x, dy, wg, wu, wd, *moments):
-    X, Y, Z = dims
     m, v = moments[:3], moments[3:]
     g = None
     for wave, (left, right) in enumerate(factors(x[0], dy[0], wg, wu, wd)):
@@ -691,10 +829,10 @@
     grads = scatter(g.reshape(MATS, *dims, 2, *UNIT), dims)
     place = lax.axis_index("dp")
     w = [lax.dynamic_slice_in_dim(a, place * b.shape[1], b.shape[1], 1) for a, b in zip((wg, wu, wd), m, strict=True)]
-    mv, out = update(grads, w, m, v, dims)
-    out = out.reshape(MATS, X, Y, Z // 2, 2, 2, *UNIT)
-    waves = [[WAVES.index((1, n) if which == 2 else (0, 2 * which + n)) for n in range(2)] for which in range(3)]
-    return (*[settle(out, pair, dims) for pair in waves], *mv)
+    flip = [jnp.swapaxes(a, 0, 1) for a in (*m, *v)]
+    mv, out = update(grads, w, flip, dims)
+    mv = [jnp.swapaxes(a, 0, 1) for a in mv]
+    return (*settle(out, dims), *mv)
 
 
 DIMS = {256: (4, 4, 8)}

time: 723 us -> 681 us (0.942); the launches traced: 714 us -> 680 us
  matrix products: 180 us -> 0 us
  Pallas kernels: 499 us -> 671 us
  local copies, waits for them, and re-layouts: 24.4 us -> 7.95 us
  other arithmetic: 8.79 us -> 0 us
    dot_general x9 -> x0, matrix products: 180 us -> none  [dotf(): return lax.dot_general(a, b, (dims, ((), ())), preferred_element_type=f32)]
    pallas_call x3 -> x4, Pallas kernels: 50.5 us -> 206 us  [the longest x3 157 us: layer_call(): pl.pallas_call(kernel, grid=(FF // WIDTH,), in_specs=[whole] * len(tokens...]
    unnamed x44 -> x22, local copies, waits for them, and re-layouts: 22.4 us -> 5.86 us
    pallas_call x6, Pallas kernels: 94.4 us -> 109 us  [product(): pl.pallas_call(functools.partial(product_kernel, kind), grid=(2, X), out_...]
where the time goes in v1:
time: 681 us; the launch traced here: 680 us
  Pallas kernels  671 us (99%)
  local copies, waits for them, and re-layouts  7.95 us (1%)
    pallas_call x1, Pallas kernels, scatter(): pl.pallas_call(functools.partial(scatter_kernel, dims, tuple(scratch)), o...  185 us
    pallas_call x1, Pallas kernels, update(): pl.pallas_call(functools.partial(update_kernel, dims, tuple(scratch)), ou...  171 us
    pallas_call x3, Pallas kernels, layer_call(): pl.pallas_call(kernel, grid=(FF // WIDTH,), in_specs=[whole] * len(tokens...  157 us
    pallas_call x6, Pallas kernels, product(): pl.pallas_call(functools.partial(product_kernel, kind), grid=(2, X), out_...  109 us
    pallas_call x1, Pallas kernels, settle(): pl.pallas_call(settle_kernel, grid=(MATS, X), out_shape=[jax.ShapeDtypeSt...  48.4 us

profile of v1, /device:TPU:1, one launch (start us, length us, event | category | flops | bytes accessed | tf_op | source)
XLA Modules:
  0.0 679.8 jit_solution(12090577944368588007)
XLA Ops:
  0.6 50.0 %bottom.1 = (bf16[1024,1536]{1,0:T(8,128)(2,1)}, f32[1024,3584]{1,0:T(8,128)}, f32[1024,3584]{1,0:T(8,128)}, bf16[1024,3584]{1,0:T(8,128)(2,1)}, bf16[1024,1536]{1,0:T(8,128)(2,1)}) custom-call(bf16[1024,1536]{1,0:T(8,128)(2,1)} %bitcast.48, bf16[2,1536,3584]{2,1,0:T(8,128)(2,1)} %wg.3, bf16[2,1536,3584]{2,1,0:T(8,128)(2,1)} %wu.3, bf16[2,3584,1536]{2,1,0:T(8,128)(2,1)} %wd.5), custom_call_target="tpu_custom_call" | custom-call | flops 33822867456 | bytes 33030144 | tf_op jit(solution)/shard_map/bottom/pallas_call | solution.py:708
  50.7 81.4 %top.1 = (bf16[1024,1536]{1,0:T(8,128)(2,1)}, bf16[1024,3584]{1,0:T(8,128)(2,1)}, bf16[1024,3584]{1,0:T(8,128)(2,1)}, bf16[1024,3584]{1,0:T(8,128)(2,1)}, bf16[1024,1536]{1,0:T(8,128)(2,1)}) custom-call(bf16[1024,1536]{1,0:T(8,128)(2,1)} %get-tuple-element.39.h, bf16[1024,1536]{1,0:T(8,128)(2,1)} %bitcast.43, bf16[2,1536,3584]{2,1,0:T(8,128)(2,1)} %wg.3, ...), custom_call_target="tpu_custom_call" | custom-call | flops 56371445760 | bytes 33030144 | tf_op jit(solution)/shard_map/top/pallas_call | solution.py:708
  132.1 25.8 %back.1 = (bf16[1024,3584]{1,0:T(8,128)(2,1)}, bf16[1024,3584]{1,0:T(8,128)(2,1)}) custom-call(bf16[1024,1536]{1,0:T(8,128)(2,1)} %get-tuple-element.40.dh.right, f32[1024,3584]{1,0:T(8,128)} %get-tuple-element.41.gate, f32[1024,3584]{1,0:T(8,128)} %get-tuple-element.42.up, bf16[2,3584,1536]{2,1,0:T(8,128)(2,1)} %wd.5), custom_call_target="tpu_custom_call" | custom-call | flops 11274289152 | bytes 11010048 | tf_op jit(solution)/shard_map/back/pallas_call | solution.py:708
  157.9 17.9 %product.6.refs_0_ = bf16[6,4,4,4,2,2,24,896]{7,6,5,4,3,2,1,0:T(8,128)(2,1)} custom-call(bf16[1024,3584]{1,0:T(8,128)(2,1)} %get-tuple-element.49.left, bf16[1024,1536]{1,0:T(8,128)(2,1)} %bitcast.44), custom_call_target="tpu_custom_call" | custom-call | flops 11274289152 | bytes 11010048 | tf_op jit(solution)/shard_map/product/pallas_call | solution.py:757
  175.8 18.3 %product.7.refs_0_ = bf16[6,4,4,4,2,2,24,896]{7,6,5,4,3,2,1,0:T(8,128)(2,1)} custom-call(bf16[1024,1536]{1,0:T(8,128)(2,1)} %get-tuple-element.46.left, bf16[1024,3584]{1,0:T(8,128)(2,1)} %get-tuple-element.48.right, bf16[6,4,4,4,2,2,24,896]{7,6,5,4,3,2,1,0:T(8,128)(2,1)} %product.6.refs_0_), custom_call_target="tpu_custom_call", output_to_operand_aliasing={{}: (2, {})} | custom-call | flops 11274289152 | bytes 11010048 | tf_op jit(solution)/shard_map/product/pallas_call | solution.py:757
  194.1 18.3 %product.8.refs_0_ = bf16[6,4,4,4,2,2,24,896]{7,6,5,4,3,2,1,0:T(8,128)(2,1)} custom-call(bf16[1024,1536]{1,0:T(8,128)(2,1)} %get-tuple-element.46.left, bf16[1024,3584]{1,0:T(8,128)(2,1)} %get-tuple-element.47.right, bf16[6,4,4,4,2,2,24,896]{7,6,5,4,3,2,1,0:T(8,128)(2,1)} %product.7.refs_0_), custom_call_target="tpu_custom_call", output_to_operand_aliasing={{}: (2, {})} | custom-call | flops 11274289152 | bytes 11010048 | tf_op jit(solution)/shard_map/product/pallas_call | solution.py:757
  212.4 17.9 %product.9.refs_0_ = bf16[6,4,4,4,2,2,24,896]{7,6,5,4,3,2,1,0:T(8,128)(2,1)} custom-call(bf16[1024,3584]{1,0:T(8,128)(2,1)} %get-tuple-element.45.left, bf16[1024,1536]{1,0:T(8,128)(2,1)} %get-tuple-element.40.dh.right, bf16[6,4,4,4,2,2,24,896]{7,6,5,4,3,2,1,0:T(8,128)(2,1)} %product.8.refs_0_), custom_call_target="tpu_custom_call", output_to_operand_aliasing={{}: (2, {})} | custom-call | flops 11274289152 | bytes 11010048 | tf_op jit(solution)/shard_map/product/pallas_call | solution.py:757
  230.4 18.3 %product.10.refs_0_ = bf16[6,4,4,4,2,2,24,896]{7,6,5,4,3,2,1,0:T(8,128)(2,1)} custom-call(bf16[1024,1536]{1,0:T(8,128)(2,1)} %get-tuple-element.38.left, bf16[1024,3584]{1,0:T(8,128)(2,1)} %get-tuple-element.44.right, bf16[6,4,4,4,2,2,24,896]{7,6,5,4,3,2,1,0:T(8,128)(2,1)} %product.9.refs_0_), custom_call_target="tpu_custom_call", output_to_operand_aliasing={{}: (2, {})} | custom-call | flops 11274289152 | bytes 11010048 | tf_op jit(solution)/shard_map/product/pallas_call | solution.py:757
  248.7 18.3 %product.11 = bf16[6,4,4,4,2,2,24,896]{7,6,5,4,3,2,1,0:T(8,128)(2,1)} custom-call(bf16[1024,1536]{1,0:T(8,128)(2,1)} %get-tuple-element.38.left, bf16[1024,3584]{1,0:T(8,128)(2,1)} %get-tuple-element.43.right, bf16[6,4,4,4,2,2,24,896]{7,6,5,4,3,2,1,0:T(8,128)(2,1)} %product.10.refs_0_), custom_call_target="tpu_custom_call", output_to_operand_aliasing={{}: (2, {})} | custom-call | flops 11274289152 | bytes 11010048 | tf_op jit(solution)/shard_map/product/pallas_call | solution.py:757
  267.0 0.0 copy-start.4
  267.0 0.0 copy-start.5
  267.0 0.0 copy-start.6
  267.0 185.4 %scatter.1 = (bf16[4,8,3584]{2,1,0:T(8,128)(2,1)}, bf16[2,16,1536]{2,1,0:T(8,128)(2,1)}, bf16[6,4,4,8,24,896]{5,4,3,2,1,0:T(8,128)(2,1)}) custom-call(bf16[6,4,4,8,2,24,896]{6,5,4,3,2,1,0:T(8,128)(2,1)} %bitcast.39), custom_call_target="tpu_custom_call" | custom-call | tf_op jit(solution)/shard_map/scatter/pallas_call | solution.py:378
  452.5 1.1 constant_dynamic-slice_fusion.1
  453.6 1.0 constant_dynamic-slice_fusion.refs_4_
  454.6 0.0 copy-done.1
  454.6 0.0 copy-done.2
  454.6 0.0 copy-done.3
  454.6 0.0 copy-done.4
  454.6 0.0 copy-done.5
  454.6 0.0 copy-done.6
  454.6 0.0 copy-start
  454.6 0.9 copy-done
  455.6 0.9 copy-done.7
  456.5 170.9 %update.1 = (f32[6,2,3584]{2,1,0:T(2,128)S(1)}, f32[6,2,3584]{2,1,0:T(2,128)S(1)}, f32[14,2,1536]{2,1,0:T(2,128)S(1)}, f32[6,2,3584]{2,1,0:T(2,128)S(1)}, f32[6,...) custom-call(bf16[4,8,3584]{2,1,0:T(8,128)(2,1)S(1)} %copy-done, ...), custom_call_target="tpu_custom_call" | custom-call | tf_op jit(solution)/shard_map/update/pallas_call | solution.py:567
  627.3 48.4 %settle.1 = (bf16[2,16,4,24,3584]{4,3,2,1,0:T(8,128)(2,1)}, bf16[2,16,4,24,3584]{4,3,2,1,0:T(8,128)(2,1)}, bf16[2,16,4,56,1536]{4,3,2,1,0:T(8,128)(2,1)}) custom-call(bf16[8,2,4,2,2,24,896]{6,5,4,3,2,1,0:T(8,128)(2,1)S(1)} %bitcast.26, bf16[8,2,4,2,2,24,896]{6,5,4,3,2,1,0:T(8,128)(2,1)S(1)} %bitcast.24, bf16[8,2,4,2,2,24,896]{6,5,4,3,2,1,0:T(8,128)(2,1)} %bitcast.42, ...), custom_call_target="tpu_custom_call" | custom-call | tf_op jit(solution)/shard_map/settle/pallas_call | solution.py:812
  675.8 0.7 copy.36
  676.4 0.7 copy.37
  677.1 0.7 copy.38
  677.8 0.7 copy.39
  678.5 0.7 copy.40
  679.1 0.7 copy.41
  (4 shorter events, 0.0 us)
Async XLA Ops:
  267.0 187.6 %copy-start.1 = (f32[2,6,3584]{2,0,1:T(2,128)S(1)}, f32[2,6,3584]{2,0,1:T(2,128)}, u32[]{:S(2)}) copy-start(f32[2,6,3584]{2,0,1:T(2,128)} %param.16) | copy-start | bytes 516100
  267.0 187.6 %copy-start.2 = (f32[2,6,3584]{2,0,1:T(2,128)S(1)}, f32[2,6,3584]{2,0,1:T(2,128)}, u32[]{:S(2)}) copy-start(f32[2,6,3584]{2,0,1:T(2,128)} %param.17) | copy-start | bytes 516100
  267.0 187.6 %copy-start.3 = (f32[2,14,1536]{2,0,1:T(2,128)S(1)}, f32[2,14,1536]{2,0,1:T(2,128)}, u32[]{:S(2)}) copy-start(f32[2,14,1536]{2,0,1:T(2,128)} %param.18) | copy-start | bytes 516100
  267.0 187.6 %copy-start.4 = (f32[2,6,3584]{2,0,1:T(2,128)S(1)}, f32[2,6,3584]{2,0,1:T(2,128)}, u32[]{:S(2)}) copy-start(f32[2,6,3584]{2,0,1:T(2,128)} %param.19) | copy-start | bytes 516100
  267.0 187.6 %copy-start.5 = (f32[2,6,3584]{2,0,1:T(2,128)S(1)}, f32[2,6,3584]{2,0,1:T(2,128)}, u32[]{:S(2)}) copy-start(f32[2,6,3584]{2,0,1:T(2,128)} %param.20) | copy-start | bytes 516100
  267.0 187.6 %copy-start.6 = (f32[2,14,1536]{2,0,1:T(2,128)S(1)}, f32[2,14,1536]{2,0,1:T(2,128)}, u32[]{:S(2)}) copy-start(f32[2,14,1536]{2,0,1:T(2,128)} %param.21) | copy-start | bytes 516100
  454.6 0.9 copy-start
  455.6 0.9 copy-start.7

commit v2 on v1

--- a/solution.py
+++ b/solution.py
@@ -13,7 +13,7 @@
 ORDERS = ("xyz", "yzx", "zxy")
 COLUMNS = ((0, 384), (384, 256), (640, 256))
 KINDS = ("s", "f", "z", "d", "e")
-SCATTER_TIMES, SCATTER_STEP = "#:LMWbb{'6CCMMXaajjs#/'85CTT]ghq", 18
+SCATTER_TIMES = '$*115::B$)-.24688;;A$()+//336<<A'
 GATHER_TIMES, GATHER_STEPS = '#-.4799Yj~#337;<DEOPQ_oi#((3@AAKX\\bgoy', (4, 14)
 MESH = pl.DeviceIdType.MESH
 START, MORE = 0, 1
@@ -129,16 +129,19 @@
 
 class Scatter:
     def __init__(self, dims):
+        self.dims = dims
+        self.X, self.Y, Z = dims
+        self.halves = Z // 2
+        self.tiles = 2 * self.X
         self.colors = [Color(k, dims) for k in range(len(ORDERS))]
         events = [e for c in self.colors for e in c.events(False)]
-        times = [time_of(c) for c in SCATTER_TIMES]
-        order = sorted(range(len(events)), key=lambda i: (times[i] % SCATTER_STEP, i))
-        self.order = [(events[i], times[i] // SCATTER_STEP) for i in order]
-        self.depth = max(lag for _, lag in self.order)
+        lag = [divmod(time_of(c), self.tiles) for c in SCATTER_TIMES]
+        self.order = [(e, *when) for e, when in zip(events, lag, strict=True)]
+        self.lag = {e: when for e, *when in self.order}
+        self.depth = max(lag for _, lag, _ in self.order)
         self.slots = self.depth + 1
-        ends = [i for i, (e, lag) in enumerate(self.order) if e[0] == "e"]
-        self.last = max(ends, key=lambda i: (self.order[i][1], i))
-        self.first = min(i for i, (e, lag) in enumerate(self.order) if e[0] == "s" and not e[2])
+        self.first = min((e for e in events if e[0] == "s" and not e[2]), key=lambda e: (*self.lag[e], events.index(e)))
+        self.last = max((e for e in events if e[0] == "e"), key=lambda e: (*self.lag[e], events.index(e)))
 
     def scratch(self):
         shapes = {}
@@ -156,13 +159,17 @@
             n = c.rings[0].n
             shapes[f"load{c.k}"] = pltpu.VMEM((n, 2) + c.block[0] + c.unit, bf16)
             shapes[f"load_sem{c.k}"] = pltpu.SemaphoreType.DMA((n, 2))
-        shapes["part_send"] = pltpu.SemaphoreType.DMA((MATS,))
+        for name in ("part_send", "own", "left_sem", "right_sem"):
+            shapes[name] = pltpu.SemaphoreType.DMA((2,))
         shapes["part_recv"] = pltpu.SemaphoreType.DMA((MATS,))
+        shapes["left"] = pltpu.VMEM((2, self.tokens, self.Y * self.halves * DOWN[0]), bf16)
+        shapes["right"] = pltpu.VMEM((2, self.tokens, 2 * UNIT[1]), bf16)
+        shapes["stage"] = pltpu.VMEM((2, self.Y, self.halves, 2, *UNIT), bf16)
         shapes["free"] = pltpu.SemaphoreType.REGULAR((MATS,))
         return shapes
 
     def lags(self, c, phase, kinds):
-        return [lag for e, lag in self.order if e[1] is c and e[2] == phase and e[0] in kinds]
+        return [lag for e, lag, _ in self.order if e[1] is c and e[2] == phase and e[0] in kinds]
 
     def kept(self, c, phase, kind):
         if kind == "s":
@@ -173,35 +180,139 @@
             ends = self.lags(c, phase + 1, "ze")
         return max(ends) - min(self.lags(c, phase, kind)) + 1
 
-    def bind(self, torus, g, pg, unit, s):
-        self.t, self.g, self.pg, self.unit, self.s = torus, g, pg, unit, s
-
-    def partner_copy(self, w):
-        t = self.t
-        return remote(self.g.at[w, :, :, :, 1 - t.core], self.pg.at[w], self.s["part_send"].at[w], self.s["part_recv"].at[w], t.partner())
-
-    def sign(self, side, w):
-        return (1 - 2 * lax.rem(w, 2)) * (1 - 2 * side)
-
-    def target(self, ring, side, j, w):
-        return self.t.wrap(ring.d, self.t.at[ring.d] + self.sign(side, w) * (ring.steps[side] - j))
-
-    def loads(self, c, side, j, w):
-        ring = c.rings[0]
-        place = ring.message(side, j) if j < ring.steps[side] else ring.n - 1
-        index = c.index(**{ring.d: self.target(ring, side, j, w)})
-        columns = (slice(None), c.columns)
-        buf, sem = self.s[f"load{c.k}"], self.s[f"load_sem{c.k}"]
-        sources = self.g.at[(w, *index, self.t.core, *columns)], self.pg.at[(w, *index, *columns)]
-        return [pltpu.make_async_copy(source, buf.at[place, n], sem.at[place, n]) for n, source in enumerate(sources)]
-
-    def start_loads(self, w):
+    def bind(self, torus, lefts, rights, g, pg, unit, s):
+        self.t, self.lefts, self.rights, self.g, self.pg, self.unit, self.s = torus, lefts, rights, g, pg, unit, s
+
+    def spot(self, d, place):
+        return lax.rem(place, 2) * self.halves + lax.div(place, 2) if d == "z" else place
+
+
+    def left(self, m, x, slot):
+        width = self.Y * self.halves * SHAPES[WAVES[m][0]][0]
+        source = self.lefts[m].at[:, pl.ds(pl.multiple_of(x * width, width), width)]
+        return pltpu.make_async_copy(source, self.s["left"].at[slot, :, pl.ds(0, width)], self.s["left_sem"].at[slot])
+
+    def right(self, m, p):
+        width = 2 * SHAPES[WAVES[m][0]][1]
+        source = self.rights[m].at[:, pl.ds(p * width, width)]
+        return pltpu.make_async_copy(source, self.s["right"].at[p, :, pl.ds(0, width)], self.s["right_sem"].at[p])
+
+    def made(self, m, p, x, slot):
+        t, s, stage = self.t, self.s, self.s["stage"]
+        place = (m, x, slice(None), pl.ds(p * self.halves, self.halves))
+        own = pltpu.make_async_copy(stage.at[slot, :, :, t.core], self.g.at[place], s["own"].at[slot])
+        return own, remote(stage.at[slot, :, :, 1 - t.core], self.pg.at[place], s["part_send"].at[slot], s["part_recv"].at[m], t.partner())
+
+    def settled(self, slot):
+        own, theirs = self.made(0, 0, 0, slot)
+        own.wait()
+        theirs.wait_send()
+
+    def multiply(self, kind, slot, p):
+        R, C = SHAPES[kind]
+        left, right, out = self.s["left"], self.s["right"], self.s["stage"]
+        for start in range(0, 2 * C, CHUNK):
+            wide = lax.dot_general(left[slot, :, 0 : self.Y * self.halves * R], right[p, :, start : start + CHUNK], (((0,), (0,)), ((), ())), preferred_element_type=f32)
+            wide = wide.reshape(self.Y, self.halves, R, CHUNK)
+            for core in range(2):
+                if kind:
+                    for natural, unit in tiles(*DOWN):
+                        at = core * C + natural[1].start - start
+                        if 0 <= at < CHUNK:
+                            rows = slice(natural[0].start, natural[0].start + natural[0].size)
+                            out[(slot, slice(None), slice(None), core, *unit)] = wide[:, :, rows, at : at + natural[1].size].astype(bf16)
+                else:
+                    begin, end = max(start, core * C), min(start + CHUNK, core * C + C)
+                    if begin < end:
+                        out[slot, :, :, core, :, begin - core * C : end - core * C] = wide[..., begin - start : end - start].astype(bf16)
+
+    def tile(self, i, j):
+        X = self.X
+        slot, p, x = lax.rem(j, 2), lax.div(j, X), lax.rem(j, X)
+        then = j + 1 == self.tiles
+        following, beside = i + then.astype(jnp.int32), jnp.where(then, 0, j + 1)
+        for m in range(MATS):
+
+            @pl.when(following == m)
+            def _():
+                self.left(m, lax.rem(beside, X), lax.rem(beside, 2)).start()
+
+            @pl.when((j == 0) & (i == m))
+            def _():
+                self.right(m, 1).start()
+
+            @pl.when((j == X) & (i + 1 == m))
+            def _():
+                self.right(m, 0).start()
+
+        @pl.when((j != 1) & (i + j > 0))
+        def _():
+            self.settled(slot)
+
+        for m, kind in enumerate(k for k, _ in WAVES[:2]):
+
+            @pl.when((lax.rem(i, 3) == 0) == (m == 0))
+            def _():
+                self.left(m, 0, slot).wait()
+
+                @pl.when(x == 0)
+                def _():
+                    self.right(m, p).wait()
+
+                self.multiply(kind, slot, p)
+
+        for copy in self.made(i, p, x, slot):
+            copy.start()
+
+    def ready(self, w):
+        self.settled(1)
+
+        @pl.when(w == MATS - 1)
+        def _():
+            self.settled(0)
+
+        s = self.s
+        remote(self.pg.at[w], self.pg.at[w], s["part_send"].at[0], s["part_recv"].at[w], self.t.partner()).wait_recv()
+        early, late = [], []
         for c in self.colors:
             ring = c.rings[0]
             for side in ring.sides:
                 for j in range(ring.steps[side] + (side == NORTH)):
-                    for copy in self.loads(c, side, j, w):
-                        copy.start()
+                    (late if self.consumer_lag(ring, side, j) else early).append((c, side, j))
+        for c, side, j in early:
+            self.start_loads(c, side, j, w)
+
+        @pl.when(w == 0)
+        def _():
+            for c, side, j in late:
+                self.start_loads(c, side, j, w)
+
+    def consumer_lag(self, ring, side, j):
+        c = ring.color
+        if j == 0:
+            e = ("s", c, 0, START, START)
+        else:
+            e = ("f", c, 0, side, j) if j < ring.steps[side] else ("z", c, 0, START, START)
+        return self.lag[e][0]
+
+    def start_loads(self, c, side, j, w):
+        for copy in self.loads(c, side, j, w):
+            copy.start()
+
+    def sign(self, side, w):
+        return (1 - 2 * lax.rem(w, 2)) * (1 - 2 * side)
+
+    def target(self, ring, side, j, w):
+        return self.t.wrap(ring.d, self.t.at[ring.d] + self.sign(side, w) * (ring.steps[side] - j))
+
+    def loads(self, c, side, j, w):
+        ring = c.rings[0]
+        place = ring.message(side, j) if j < ring.steps[side] else ring.n - 1
+        index = c.index(**{ring.d: self.spot(ring.d, self.target(ring, side, j, w))})
+        columns = (slice(None), c.columns)
+        buf, sem = self.s[f"load{c.k}"], self.s[f"load_sem{c.k}"]
+        sources = self.g.at[(w, *index, *columns)], self.pg.at[(w, *index, *columns)]
+        return [pltpu.make_async_copy(source, buf.at[place, n], sem.at[place, n]) for n, source in enumerate(sources)]
 
     def message(self, ring, side, m, w, src):
         s, name = self.s, ring.name
@@ -212,19 +323,18 @@
         c, s = ring.color, self.s
         if ring.phase:
             before = s["sum" + c.rings[0].name]
-            own = [(before, (lax.rem(w, before.shape[0]), *c.within(self.target(ring, side, j, w))))]
+            own = [(before, (lax.rem(w, before.shape[0]), *c.within(self.spot(ring.d, self.target(ring, side, j, w)))))]
         else:
             place = ring.message(side, j) if j < ring.steps[side] else ring.n - 1
             for copy in self.loads(c, side, j, w):
                 copy.wait()
             own = [(s[f"load{c.k}"], (place, n)) for n in range(2)]
         add_blocks(dst, index, own + terms, c.block[ring.phase])
-        if not ring.phase:
+        if not ring.phase and self.consumer_lag(ring, side, j):
 
             @pl.when(w + 1 < MATS)
             def _():
-                for copy in self.loads(c, side, j, w + 1):
-                    copy.start()
+                self.start_loads(c, side, j, w + 1)
 
     def event(self, kind, c, phase, side, j, w):
         ring, s = c.rings[phase], self.s
@@ -257,10 +367,10 @@
             copies = [direct(self.t, ring, o, w, out.at[part, o - 1], box.at[slot, o - 1], s, slot, slot) for o in range(1, ring.n)]
             if kind == "d":
                 for o, copy in enumerate(copies):
-                    out[part, o] = total[last, self.t.wrap(ring.d, self.t.at[ring.d] + o + 1)].astype(bf16)
+                    out[part, o] = total[last, self.spot(ring.d, self.t.wrap(ring.d, self.t.at[ring.d] + o + 1))].astype(bf16)
                     copy.start()
             else:
-                value = total[last, self.t.at[ring.d]]
+                value = total[last, self.spot(ring.d, self.t.at[ring.d])]
                 for o, copy in enumerate(copies):
                     copy.wait_recv()
                     value = value + box[slot, o].astype(f32)
@@ -268,45 +378,51 @@
                 for copy in copies:
                     copy.wait_send()
 
-    def step(self, i):
-        @pl.when(i + 1 < MATS)
+    def step(self, i, j):
+        @pl.when(i < MATS)
         def _():
-            self.partner_copy(i + 1).wait_recv()
-
-        for n, (e, lag) in enumerate(self.order):
-            w = i - lag
-
-            @pl.when((w >= 0) & (w < MATS))
+            self.tile(i, j)
+
+        @pl.when((j == 0) & (i > 0) & (i <= MATS))
+        def _():
+            self.ready(i - 1)
+
+        for at in range(self.tiles):
+
+            @pl.when(j == at)
             def _():
-                if n == self.first:
-
-                    @pl.when(w >= self.slots)
-                    def _():
-                        pl.semaphore_wait(self.s["free"].at[w - self.slots], len(self.t.everyone()))
-
-                self.event(*e, w)
-                if n == self.last:
-
-                    @pl.when(w + self.slots < MATS)
-                    def _():
-                        for device in self.t.everyone():
-                            signal(self.s["free"].at[w], device)
+                for e, lag, _ in sorted((n for n in self.order if n[2] == at), key=lambda n: n[1]):
+                    self.turn(e, i - 1 - lag)
+
+    def turn(self, e, w):
+        @pl.when((w >= 0) & (w < MATS))
+        def _():
+            if e == self.first:
+
+                @pl.when(w >= self.slots)
+                def _():
+                    pl.semaphore_wait(self.s["free"].at[w - self.slots], len(self.t.everyone()))
+
+            self.event(*e, w)
+            if e == self.last:
+
+                @pl.when(w + self.slots < MATS)
+                def _():
+                    for device in self.t.everyone():
+                        signal(self.s["free"].at[w], device)
 
     def run(self):
-        for w in range(MATS):
-            self.partner_copy(w).start()
-        self.partner_copy(0).wait_recv()
-        self.start_loads(0)
-
-        def body(i, _):
-            self.step(i)
+        self.left(0, 0, 0).start()
+        self.right(0, 0).start()
+
+        def body(n, _):
+            self.step(lax.div(n, self.tiles), lax.rem(n, self.tiles))
             return 0
 
-        lax.fori_loop(0, MATS + self.depth, body, 0)
-        for w in range(MATS):
-            self.partner_copy(w).wait_send()
-
-
+        lax.fori_loop(0, (MATS + self.slots) * self.tiles, body, 0)
+
+
+CHUNK = 256
 WAVES = ((1, 1), (0, 1), (0, 3), (1, 0), (0, 0), (0, 2))
 SHAPES = (UNIT, DOWN)
 
@@ -345,12 +461,15 @@
         copy.wait()
 
 
-def scatter_kernel(dims, names, g, *refs):
-    outs, pg, s = refs[:2], refs[2], dict(zip(names, refs[3:], strict=True))
+def scatter_kernel(dims, names, *refs):
+    take = iter(refs)
+    lefts, rights, outs = ([next(take) for _ in range(n)] for n in (MATS, MATS, 2))
+    g, pg = next(take), next(take)
+    s = dict(zip(names, take, strict=True))
     t = Torus(dims)
     t.enter()
     sc = Scatter(dims)
-    sc.bind(t, g, pg, s["unit"], s)
+    sc.bind(t, lefts, rights, g, pg, s["unit"], s)
     sc.run()
     for w, (kind, at) in enumerate(WAVES):
         R, C = SHAPES[kind]
@@ -371,19 +490,22 @@
     return pl.BlockSpec(memory_space=pl.ANY), pl.BlockSpec(memory_space=pltpu.VMEM)
 
 
-def scatter(g, dims):
-    scratch = Scatter(dims).scratch() | {"unit": pltpu.VMEM((MATS, *UNIT), f32)} | exchange_scratch()
+def scatter(factors, dims):
+    sc = Scatter(dims)
+    sc.tokens = factors[0][0].shape[0]
+    scratch = sc.scratch() | {"unit": pltpu.VMEM((MATS, *UNIT), f32)} | exchange_scratch()
     anywhere, vmem = places()
     rows = [jax.ShapeDtypeStruct((sum(w[0] == kind for w in WAVES), PADS[kind], 4 * C), bf16) for kind, (_, C) in enumerate(SHAPES)]
-    *grads, _ = pl.pallas_call(
+    terms = jax.ShapeDtypeStruct((MATS, *dims, *UNIT), bf16)
+    *grads, _, _ = pl.pallas_call(
         functools.partial(scatter_kernel, dims, tuple(scratch)),
-        out_shape=(*rows, jax.ShapeDtypeStruct((MATS, *dims, *UNIT), bf16)),
-        in_specs=[anywhere],
-        out_specs=(vmem, vmem, anywhere),
+        out_shape=(*rows, terms, terms),
+        in_specs=[anywhere] * 2 * MATS,
+        out_specs=(vmem, vmem, anywhere, anywhere),
         scratch_shapes=list(scratch.values()),
         compiler_params=pltpu.CompilerParams(collective_id=1, has_side_effects=True, vmem_limit_bytes=VMEM_MOST),
         name="scatter",
-    )(g)
+    )(*[left for left, _ in factors], *[right for _, right in factors])
     return grads
 
 
@@ -726,48 +848,6 @@
     return (hid1, dy), (a1, dg1), (a1, du1), (hid0, dh), (a0, dg0), (a0, du0)
 
 
-def product_kernel(kind, left, right, *refs):
-    out = refs[-1]
-    C, width = SHAPES[kind][1], out.shape[5] * SHAPES[kind][1]
-    for start in range(0, width, CHUNK):
-        wide = lax.dot_general(left[...], right[:, start : start + CHUNK], (((0,), (0,)), ((), ())), preferred_element_type=f32)
-        wide = wide.reshape(out.shape[2], out.shape[3], SHAPES[kind][0], CHUNK)
-        if kind:
-            for natural, unit in tiles(*DOWN):
-                for core in range(out.shape[5]):
-                    at = core * C + natural[1].start - start
-                    if 0 <= at < CHUNK:
-                        out[(0, 0, slice(None), slice(None), 0, core, *unit)] = wide[:, :, natural[0].start : natural[0].start + natural[0].size, at : at + natural[1].size].astype(bf16)
-        else:
-            for core in range(out.shape[5]):
-                begin, end = max(start, core * C), min(start + CHUNK, core * C + C)
-                if begin < end:
-                    out[0, 0, :, :, 0, core, :, begin - core * C : end - core * C] = wide[..., begin - start : end - start].astype(bf16)
-
-
-CHUNK = 256
-
-
-def product(wave, left, right, into, dims):
-    X, Y, Z = dims
-    kind = WAVES[wave][0]
-    R, C = SHAPES[kind]
-    tokens, halves = right.shape[0], Z // 2
-    given = [] if into is None else [into]
-    return pl.pallas_call(
-        functools.partial(product_kernel, kind),
-        grid=(2, X),
-        out_shape=jax.ShapeDtypeStruct((MATS, X, Y, halves, 2, 2, *UNIT), bf16),
-        in_specs=[pl.BlockSpec((tokens, R * Y * halves), lambda p, i: (0, i)), pl.BlockSpec((tokens, 2 * C), lambda p, i: (0, p))]
-        + [pl.BlockSpec(memory_space=pl.ANY)] * len(given),
-        out_specs=pl.BlockSpec((1, 1, Y, halves, 1, 2, *UNIT), lambda p, i: (wave, i, 0, 0, p, 0, 0, 0)),
-        input_output_aliases={2: 0} if given else {},
-        cost_estimate=pl.CostEstimate(flops=2 * left.size * right.shape[1], bytes_accessed=2 * left.shape[1] * right.shape[1], transcendentals=0),
-        compiler_params=pltpu.CompilerParams(vmem_limit_bytes=VMEM_MOST),
-        name="product",
-    )(left, right, *given)
-
-
 SETTLED = (4, 1, 5, 2, 3, 0)
 SHARE = 2
 
@@ -823,10 +903,7 @@
 
 def device_step(dims, x, dy, wg, wu, wd, *moments):
     m, v = moments[:3], moments[3:]
-    g = None
-    for wave, (left, right) in enumerate(factors(x[0], dy[0], wg, wu, wd)):
-        g = product(wave, left, right, g, dims)
-    grads = scatter(g.reshape(MATS, *dims, 2, *UNIT), dims)
+    grads = scatter(factors(x[0], dy[0], wg, wu, wd), dims)
     place = lax.axis_index("dp")
     w = [lax.dynamic_slice_in_dim(a, place * b.shape[1], b.shape[1], 1) for a, b in zip((wg, wu, wd), m, strict=True)]
     flip = [jnp.swapaxes(a, 0, 1) for a in (*m, *v)]

time: 681 us -> 580 us (0.85)
  Pallas kernels: 671 us -> 571 us
    pallas_call x6 -> x0, Pallas kernels: 109 us -> none  [product(): pl.pallas_call(functools.partial(product_kernel, kind), grid=(2, X), out_...]
    pallas_call x1, Pallas kernels: 185 us -> 197 us  [scatter(): pl.pallas_call(functools.partial(scatter_kernel, dims, tuple(scratch)), o...]
where the time goes in v2:
time: 580 us; the launch traced here: 579 us
  Pallas kernels  571 us (98%)
  local copies, waits for them, and re-layouts  7.95 us (1%)
    pallas_call x1, Pallas kernels, scatter(): pl.pallas_call(functools.partial(scatter_kernel, dims, tuple(scratch)), o...  197 us
    pallas_call x1, Pallas kernels, update(): pl.pallas_call(functools.partial(update_kernel, dims, tuple(scratch)), ou...  168 us
    pallas_call x3, Pallas kernels, layer_call(): pl.pallas_call(kernel, grid=(FF // WIDTH,), in_specs=[whole] * len(tokens...  157 us
    pallas_call x1, Pallas kernels, settle(): pl.pallas_call(settle_kernel, grid=(MATS, X), out_shape=[jax.ShapeDtypeSt...  48.4 us

profile of v2, /device:TPU:1, one launch (start us, length us, event | category | flops | bytes accessed | tf_op | source)
XLA Modules:
  0.0 579.3 jit_solution(12038537876661909923)
XLA Ops:
  0.6 1.0 constant_dynamic-slice_fusion.refs_4_
  1.6 1.1 constant_dynamic-slice_fusion.1
  2.7 50.0 %bottom.1 = (bf16[1024,1536]{1,0:T(8,128)(2,1)}, f32[1024,3584]{1,0:T(8,128)}, f32[1024,3584]{1,0:T(8,128)}, bf16[1024,3584]{1,0:T(8,128)(2,1)}, bf16[1024,1536]{1,0:T(8,128)(2,1)}) custom-call(bf16[1024,1536]{1,0:T(8,128)(2,1)} %bitcast.46, bf16[2,1536,3584]{2,1,0:T(8,128)(2,1)} %wg.3, bf16[2,1536,3584]{2,1,0:T(8,128)(2,1)} %wu.3, bf16[2,3584,1536]{2,1,0:T(8,128)(2,1)} %wd.5), custom_call_target="tpu_custom_call" | custom-call | flops 33822867456 | bytes 33030144 | tf_op jit(solution)/shard_map/bottom/pallas_call | solution.py:830
  52.8 81.4 %top.1 = (bf16[1024,1536]{1,0:T(8,128)(2,1)}, bf16[1024,3584]{1,0:T(8,128)(2,1)}, bf16[1024,3584]{1,0:T(8,128)(2,1)}, bf16[1024,3584]{1,0:T(8,128)(2,1)}, bf16[1024,1536]{1,0:T(8,128)(2,1)}) custom-call(bf16[1024,1536]{1,0:T(8,128)(2,1)} %get-tuple-element.38.h, bf16[1024,1536]{1,0:T(8,128)(2,1)} %bitcast.41, bf16[2,1536,3584]{2,1,0:T(8,128)(2,1)} %wg.3, ...), custom_call_target="tpu_custom_call" | custom-call | flops 56371445760 | bytes 33030144 | tf_op jit(solution)/shard_map/top/pallas_call | solution.py:830
  134.2 25.9 %back.1 = (bf16[1024,3584]{1,0:T(8,128)(2,1)}, bf16[1024,3584]{1,0:T(8,128)(2,1)}) custom-call(bf16[1024,1536]{1,0:T(8,128)(2,1)} %get-tuple-element.45.dh.refs_9_, f32[1024,3584]{1,0:T(8,128)} %get-tuple-element.46.gate, f32[1024,3584]{1,0:T(8,128)} %get-tuple-element.47.up, bf16[2,3584,1536]{2,1,0:T(8,128)(2,1)} %wd.5), custom_call_target="tpu_custom_call" | custom-call | flops 11274289152 | bytes 11010048 | tf_op jit(solution)/shard_map/back/pallas_call | solution.py:830
  160.1 0.0 copy-start.1
  160.1 0.0 copy-start.2
  160.1 0.0 copy-start.3
  160.1 0.0 copy-start.4
  160.1 0.0 copy-start.5
  160.1 0.0 copy-start.6
  160.1 196.7 %scatter.1 = (bf16[4,8,3584]{2,1,0:T(8,128)(2,1)}, bf16[2,16,1536]{2,1,0:T(8,128)(2,1)}, bf16[6,4,4,8,24,896]{5,4,3,2,1,0:T(8,128)(2,1)}, bf16[6,4,4,8,24,896]{5,4,3,2,1,0:T(8,128)(2,1)}) custom-call(bf16[1024,3584]{1,0:T(8,128)(2,1)} %get-tuple-element.39.refs_0_, bf16[1024,1536]{1,0:T(8,128)(2,1)} %get-tuple-element.40.refs_1_.refs_2_, ...), custom_call_target="tpu_custom_call" | custom-call | tf_op jit(solution)/shard_map/scatter/pallas_call | solution.py:500
  356.8 0.0 copy-done.1
  356.8 0.0 copy-done.2
  356.8 0.0 copy-done.3
  356.8 0.0 copy-done.4
  356.8 0.0 copy-done.5
  356.8 0.0 copy-done.6
  356.9 0.0 copy-start
  356.9 0.9 copy-done
  357.8 0.0 copy-start.7
  357.8 0.9 copy-done.7
  358.7 168.1 %update.1 = (f32[6,2,3584]{2,1,0:T(2,128)S(1)}, f32[6,2,3584]{2,1,0:T(2,128)S(1)}, f32[14,2,1536]{2,1,0:T(2,128)S(1)}, f32[6,2,3584]{2,1,0:T(2,128)S(1)}, f32[6,...) custom-call(bf16[4,8,3584]{2,1,0:T(8,128)(2,1)S(1)} %copy-done, ...), custom_call_target="tpu_custom_call" | custom-call | tf_op jit(solution)/shard_map/update/pallas_call | solution.py:689
  526.8 48.4 %settle.1 = (bf16[2,16,4,24,3584]{4,3,2,1,0:T(8,128)(2,1)}, bf16[2,16,4,24,3584]{4,3,2,1,0:T(8,128)(2,1)}, bf16[2,16,4,56,1536]{4,3,2,1,0:T(8,128)(2,1)}) custom-call(bf16[8,2,4,2,2,24,896]{6,5,4,3,2,1,0:T(8,128)(2,1)S(1)} %bitcast.25, bf16[8,2,4,2,2,24,896]{6,5,4,3,2,1,0:T(8,128)(2,1)S(1)} %bitcast.23, bf16[8,2,4,2,2,24,896]{6,5,4,3,2,1,0:T(8,128)(2,1)} %bitcast.40, ...), custom_call_target="tpu_custom_call" | custom-call | tf_op jit(solution)/shard_map/settle/pallas_call | solution.py:892
  575.3 0.7 copy.26
  575.9 0.7 copy.27
  576.6 0.7 copy.28
  577.3 0.7 copy.29
  577.9 0.7 copy.30
  578.6 0.7 copy.31
Async XLA Ops:
  160.1 196.7 %copy-start.1 = (f32[2,6,3584]{2,0,1:T(2,128)S(1)}, f32[2,6,3584]{2,0,1:T(2,128)}, u32[]{:S(2)}) copy-start(f32[2,6,3584]{2,0,1:T(2,128)} %param.16) | copy-start | bytes 516100
  160.1 196.7 %copy-start.2 = (f32[2,6,3584]{2,0,1:T(2,128)S(1)}, f32[2,6,3584]{2,0,1:T(2,128)}, u32[]{:S(2)}) copy-start(f32[2,6,3584]{2,0,1:T(2,128)} %param.17) | copy-start | bytes 516100
  160.1 196.7 %copy-start.3 = (f32[2,14,1536]{2,0,1:T(2,128)S(1)}, f32[2,14,1536]{2,0,1:T(2,128)}, u32[]{:S(2)}) copy-start(f32[2,14,1536]{2,0,1:T(2,128)} %param.18) | copy-start | bytes 516100
  160.1 196.7 %copy-start.4 = (f32[2,6,3584]{2,0,1:T(2,128)S(1)}, f32[2,6,3584]{2,0,1:T(2,128)}, u32[]{:S(2)}) copy-start(f32[2,6,3584]{2,0,1:T(2,128)} %param.19) | copy-start | bytes 516100
  160.1 196.7 %copy-start.5 = (f32[2,6,3584]{2,0,1:T(2,128)S(1)}, f32[2,6,3584]{2,0,1:T(2,128)}, u32[]{:S(2)}) copy-start(f32[2,6,3584]{2,0,1:T(2,128)} %param.20) | copy-start | bytes 516100
  160.1 196.7 %copy-start.6 = (f32[2,14,1536]{2,0,1:T(2,128)S(1)}, f32[2,14,1536]{2,0,1:T(2,128)}, u32[]{:S(2)}) copy-start(f32[2,14,1536]{2,0,1:T(2,128)} %param.21) | copy-start | bytes 516100
  356.9 0.9 copy-start
  357.8 0.9 copy-start.7

commit v3 on v2

--- a/solution.py
+++ b/solution.py
@@ -50,13 +50,15 @@
     def group(self, s):
         return (self.rep, self.idx - lax.rem(self.idx, 4) + s)
 
-    def enter(self):
-        me = lax.rem(self.idx, 4)
-        barrier = pltpu.get_barrier_semaphore()
-        devices = self.everyone() + [self.partner(), self.group(lax.rem(me + 3 - 2 * self.core, 4))]
-        for device in devices:
-            signal(barrier, device)
-        pl.semaphore_wait(barrier, len(devices))
+    def crossed(self):
+        return self.group(lax.rem(lax.rem(self.idx, 4) + 3 - 2 * self.core, 4))
+
+
+def enter(devices):
+    barrier = pltpu.get_barrier_semaphore()
+    for device in devices:
+        signal(barrier, device)
+    pl.semaphore_wait(barrier, len(devices))
 
 
 def signal(sem, device):
@@ -467,7 +469,7 @@
     g, pg = next(take), next(take)
     s = dict(zip(names, take, strict=True))
     t = Torus(dims)
-    t.enter()
+    enter(t.everyone() + [t.partner(), t.crossed()])
     sc = Scatter(dims)
     sc.bind(t, lefts, rights, g, pg, s["unit"], s)
     sc.run()
@@ -599,56 +601,66 @@
             self.finish(w)
 
 
-AXES = ("core", "x", "y", "z")
-
-
-def sum_over_all(t, s, value):
-    for n, d in enumerate(AXES):
-        mine, box = s["norm_out"].at[n], s["norm_" + d]
-        mine[...] = value
-        copies = []
-        for o in range(box.shape[0]):
-            device = t.partner() if d == "core" else t.beside(d, o + 1)
-            copies.append(remote(mine, box.at[o], s["norm_send"].at[n, o], s["norm_recv"].at[n, o], device))
-        for copy in copies:
-            copy.start()
-        for copy in copies:
-            copy.wait()
-        for o in range(box.shape[0]):
-            value = value + box[o]
-    return value
+class Exchange:
+    def __init__(self, t, dims):
+        X, Y, Z = dims
+        near = t.cores * Z
+        self.t, self.steps = t, ((near, 1, near), (X * Y, near, X * Y))
+
+    def beside(self, n, offset):
+        size, stride, _ = self.steps[n]
+        idx = self.t.idx
+        at = lax.rem(lax.div(idx, stride), size)
+        return (self.t.rep, idx + (lax.rem(at + offset, size) - at) * stride)
+
+    def devices(self):
+        return [self.beside(n, o) for n, (size, *_) in enumerate(self.steps) for o in range(1, size)]
+
+    def total(self, s, value):
+        for n, (size, *_) in enumerate(self.steps):
+            mine, box = s["norm_out"].at[n], s["norm_in"].at[n]
+            mine[...] = value
+            copies = [remote(mine, box.at[o], s["norm_send"].at[n, o], s["norm_recv"].at[n, o], self.beside(n, o)) for o in range(1, size)]
+            for copy in copies:
+                copy.start()
+            for copy in copies:
+                copy.wait()
+            value = value + sum(box[o] for o in range(1, size))
+        return value
+
+
+def moments_of(g, m, v):
+    return 0.9 * m + 0.1 * g, 0.95 * v + 0.05 * g * g
+
+
+def rows_of(grads, kind, at):
+    which, layer = (2, at) if kind else divmod(at, 2)
+    return grads[kind][at, 0 : SHAPES[kind][0] // 4, :].astype(f32), which, layer
 
 
 def update_kernel(dims, names, *refs):
     take = iter(refs)
-    grads, w_in, m_in, v_in, m_out, v_out = ([next(take) for _ in range(n)] for n in (2, 3, 3, 3, 3, 3))
-    out = [next(take) for _ in WAVES]
+    grads, w_in, m_in, v_in = ([next(take) for _ in range(n)] for n in (2, 3, 3, 3))
+    factor_out, out = next(take), [next(take) for _ in WAVES]
     s = dict(zip(names, take, strict=True))
     t = Torus(dims)
-    t.enter()
-
-    def rows(kind, at):
-        return grads[kind][at, 0 : SHAPES[kind][0] // 4, :].astype(f32)
-
+    ex = Exchange(t, dims)
+    enter(ex.devices())
     total, count = jnp.zeros((1, 1), f32), 0
     for kind, at in WAVES:
-        g = rows(kind, at)
+        g, *_ = rows_of(grads, kind, at)
+        total = total + jnp.sum(jnp.sum(g * g, axis=0, keepdims=True), axis=1, keepdims=True)
         count += g.size
-        total = total + jnp.sum(jnp.sum(g * g, axis=0, keepdims=True), axis=1, keepdims=True)
-    for d in AXES:
-        count *= s["norm_" + d].shape[0] + 1
-    total = sum_over_all(t, s, jnp.broadcast_to(total, TILE))[0:1, 0:1]
-    factor = jnp.minimum(1.0, 0.5 * lax.rsqrt(total / count + 1e-30))
-
+    for size, *_ in ex.steps:
+        count *= size
+    total = ex.total(s, jnp.broadcast_to(total, TILE))
+    factor_out[...] = jnp.minimum(1.0, 0.5 * lax.rsqrt(total / count + 1e-30))
+    factor = factor_out[0:1, 0:1]
     for kind, at in WAVES:
-        which, layer = (2, at) if kind else divmod(at, 2)
+        g, which, layer = rows_of(grads, kind, at)
         R, C = SHAPES[kind]
-        g = rows(kind, at) * factor
         w = w_in[which][layer].astype(f32)
-        m = 0.9 * m_in[which][:, layer, :] + 0.1 * g
-        v = 0.95 * v_in[which][:, layer, :] + 0.05 * g * g
-        m_out[which][:, layer, :] = m
-        v_out[which][:, layer, :] = v
+        m, v = moments_of(g * factor, m_in[which][:, layer, :], v_in[which][:, layer, :])
         w = (w - 0.02 * (m * lax.rsqrt(v + 1e-8) + 0.1 * w)).astype(bf16)
         for q in range(4):
             s[f"slab{kind}"][q, at, 0 : R // 4, :] = w[:, C * q : C * (q + 1)]
@@ -667,7 +679,7 @@
     ga.run()
 
 
-IN_VMEM = (1, 2, 4)
+IN_VMEM = (0, 1, 2, 3)
 
 
 def home(wave):
@@ -675,31 +687,30 @@
 
 
 def update(grads, w, moments, dims):
+    X, Y, Z = dims
     scratch = Gather(dims).scratch() | exchange_scratch()
     scratch["unit"] = pltpu.VMEM((MATS, *UNIT), bf16)
     scratch["wide"] = pltpu.VMEM(UNIT, f32)
-    scratch["norm_out"] = pltpu.VMEM((len(AXES), *TILE), f32)
-    for d, n in zip(AXES, (2, *dims), strict=True):
-        scratch["norm_" + d] = pltpu.VMEM((n - 1, *TILE), f32)
+    most = max(2 * Z, X * Y)
+    scratch["norm_out"] = pltpu.VMEM((2, *TILE), f32)
+    scratch["norm_in"] = pltpu.VMEM((2, most, *TILE), f32)
     for name in ("norm_send", "norm_recv"):
-        scratch[name] = pltpu.SemaphoreType.DMA((len(AXES), max(dims)))
+        scratch[name] = pltpu.SemaphoreType.DMA((2, most))
     anywhere, vmem = places()
     given = (*grads, *w, *moments)
-    like = [jax.ShapeDtypeStruct(a.shape, f32) for a in moments]
-    results = pl.pallas_call(
+    factor, *out = pl.pallas_call(
         functools.partial(update_kernel, dims, tuple(scratch)),
-        out_shape=like + [home(w)((*dims, 2, *UNIT), bf16) for w in range(MATS)],
+        out_shape=[jax.ShapeDtypeStruct(TILE, f32)] + [home(wave)((*dims, 2, *UNIT), bf16) for wave in range(MATS)],
         in_specs=[vmem] * len(given),
-        out_specs=[vmem] * len(like) + [anywhere] * MATS,
+        out_specs=[vmem] + [anywhere] * MATS,
         scratch_shapes=list(scratch.values()),
         compiler_params=pltpu.CompilerParams(collective_id=2, has_side_effects=True, vmem_limit_bytes=VMEM_FEW),
         name="update",
     )(*given)
-    return results[: len(like)], results[len(like) :]
-
-
-VMEM_MOST, VMEM_SOME, VMEM_FEW = 62 << 20, 40 << 20, 12 << 20
-VMEM_HALF = 20 << 20
+    return factor, out
+
+
+VMEM_MOST, VMEM_FEW = 62 << 20, 12 << 20
 
 
 def normed(h):
@@ -743,6 +754,7 @@
     def _():
         def first(rows):
             a[rows] = normed(h[rows])
+            acc[rows] = jnp.zeros_like(acc[rows])
 
         by_rows(h, first)
 
@@ -750,15 +762,7 @@
         gate[:, part] = dot(a[...], wg[0, :, part], PLAIN)
         up[:, part] = dot(a[...], wu[0, :, part], PLAIN)
         hid[:, part] = (jax.nn.silu(gate[:, part]) * up[:, part]).astype(bf16)
-    term = dot(hid[...], wd[0], PLAIN)
-
-    @pl.when(step == 0)
-    def _():
-        acc[...] = term
-
-    @pl.when(step > 0)
-    def _():
-        acc[...] += term
+    acc[...] += dot(hid[...], wd[0], PLAIN)
 
     @pl.when(step == pl.num_programs(0) - 1)
     def _():
@@ -775,6 +779,8 @@
     def _():
         def first(rows):
             a[rows] = normed(h[rows])
+            for acc in (acc_gate, acc_up):
+                acc[rows] = jnp.zeros_like(acc[rows])
 
         by_rows(h, first)
 
@@ -786,15 +792,7 @@
         by_gate, by_up = gate_back(dhid, gate, up)
         dgate[:, part], dup[:, part] = by_gate.astype(bf16), by_up.astype(bf16)
     for acc, d, w in ((acc_gate, dgate, wg), (acc_up, dup, wu)):
-        term = dot(d[...], w[0], TURNED)
-
-        @pl.when(step == 0)
-        def _():
-            acc[...] = term
-
-        @pl.when(step > 0)
-        def _():
-            acc[...] += term
+        acc[...] += dot(d[...], w[0], TURNED)
 
     @pl.when(step == pl.num_programs(0) - 1)
     def _():
@@ -849,67 +847,95 @@
 
 
 SETTLED = (4, 1, 5, 2, 3, 0)
-SHARE = 2
+BOXES = 3
+
+
+def pieces(kind):
+    runs = []
+    for (rows, columns), (unit_rows, unit_columns) in tiles(*SHAPES[kind]):
+        if runs and runs[-1][:2] == [rows, unit_rows]:
+            runs[-1][-1] += columns.size
+        else:
+            runs.append([rows, unit_rows, columns.start, unit_columns.start, columns.size])
+    return runs
 
 
 def settle_kernel(*refs):
-    step = pl.program_id(0)
-    for n, (wave, w) in enumerate(zip(SETTLED, refs)):
-        kind, out = WAVES[wave][0], refs[MATS + n // 2]
+    take = iter(refs)
+    waves, grads, m_in, v_in, outs, m_out, v_out = ([next(take) for _ in range(n)] for n in (MATS, 2, 3, 3, 3, 3, 3))
+    factor, box, in_sem, out_sem, near_sem = next(take), *take
+    X = waves[0].shape[0]
+
+    def put(n, x, q, block, sem):
+        kind = WAVES[SETTLED[n]][0]
         C = SHAPES[kind][1]
-
-        @pl.when(step == n)
-        def _():
-            for q in range(4):
-                block = w.at[0, :, :, q // 2, q % 2]
-                if kind:
-                    for natural, unit in tiles(*DOWN):
-                        out[:, :, :, natural[0], pl.ds(C * q + natural[1].start, natural[1].size)] = block[(slice(None), slice(None), *unit)][None]
-                else:
-                    out[:, :, :, :, C * q : C * (q + 1)] = block[...][None]
-
-
-def settle(waves, dims):
+        for rows, unit_rows, column, unit_column, width in pieces(kind):
+            to = outs[n // 2].at[n % 2, x, :, :, rows, pl.ds(pl.multiple_of(C * q + column, TILE[1]), width)]
+            pltpu.make_async_copy(block.at[:, :, lax.div(q, 2), lax.rem(q, 2), unit_rows, pl.ds(unit_column, width)], to, sem).start()
+
+    def all_of(n, x, block, sem):
+        lax.fori_loop(0, 4, lambda q, _: (put(n, x, q, block, sem), 0)[1], 0)
+
+    near = [n for n, w in enumerate(SETTLED) if w in IN_VMEM]
+    far = [(n, x) for n in range(MATS) if n not in near for x in range(X)]
+
+    def fetch(k):
+        n, x = far[k]
+        return pltpu.make_async_copy(waves[n].at[x], box.at[k % BOXES], in_sem.at[k % BOXES])
+
+    def drain(k):
+        n, x = far[k]
+        pltpu.make_async_copy(box.at[k % BOXES], waves[n].at[x], out_sem.at[k % BOXES]).wait()
+
+    ahead = BOXES - 1
+    for k in range(ahead):
+        fetch(k).start()
+    for n in near:
+        lax.fori_loop(0, X, lambda x, _: (all_of(n, x, waves[n].at[x], near_sem.at[n]), 0)[1], 0)
+    for kind, at in WAVES:
+        g, which, layer = rows_of(grads, kind, at)
+        m, v = moments_of(g * factor[0:1, 0:1], m_in[which][:, layer, :], v_in[which][:, layer, :])
+        m_out[which][:, layer, :], v_out[which][:, layer, :] = m, v
+    for k in range(len(far)):
+        fetch(k).wait()
+        all_of(*far[k], box.at[k % BOXES], out_sem.at[k % BOXES])
+        if k + ahead < len(far):
+            if k:
+                drain(k - 1)
+            fetch(k + ahead).start()
+    for k in range(len(far) - BOXES, len(far)):
+        drain(k)
+    for n in near:
+        pltpu.make_async_copy(waves[n], waves[n], near_sem.at[n]).wait()
+
+
+def settle(waves, factor, grads, moments, dims):
     X, Y, Z = dims
-    X, Y, halves = X * SHARE, Y // SHARE, Z // 2
-    shape = (Y, halves, 2, 2, *UNIT)
-
-    def turn(first, last, n, i):
-        return jnp.clip((n - first) * X + i, 0, (last - first + 1) * X - 1)
-
-    def given(n):
-        return pl.BlockSpec((1, *shape), lambda k, i: (turn(n, n, k, i), *[0] * len(shape)))
-
-    def made(which):
-        R, C = SHAPES[which // 2]
-
-        def place(k, i):
-            at = turn(2 * which, 2 * which + 1, k, i)
-            return (at // X, at % X, 0, 0, 0)
-
-        return pl.BlockSpec((1, Y, halves, R, 4 * C), place)
-
+    halves = Z // 2
+    shape = (X, Y, halves, 2, 2, *UNIT)
+    anywhere, vmem = places()
+    made = jax.ShapeDtypeStruct
+    R, C = zip(*SHAPES)
     outs = pl.pallas_call(
-        settle_kernel,
-        grid=(MATS, X),
-        out_shape=[jax.ShapeDtypeStruct((2, X * Y, halves, SHAPES[which // 2][0], 4 * SHAPES[which // 2][1]), bf16) for which in range(3)],
-        in_specs=[given(n) for n in range(MATS)],
-        out_specs=[made(which) for which in range(3)],
-        compiler_params=pltpu.CompilerParams(vmem_limit_bytes=VMEM_HALF),
+        lambda *refs: settle_kernel(*refs[: MATS + 2 + len(moments)], *refs[MATS + 3 + len(moments) : -4], refs[MATS + 2 + len(moments)], *refs[-4:]),
+        out_shape=[made((2, X, Y, halves, R[which // 2], 4 * C[which // 2]), bf16) for which in range(3)] + [made(a.shape, f32) for a in moments],
+        in_specs=[vmem if n in IN_VMEM else anywhere for n in SETTLED] + [vmem] * (3 + len(moments)),
+        out_specs=[anywhere] * 3 + [vmem] * len(moments),
+        scratch_shapes=[pltpu.VMEM((BOXES, *shape[1:]), bf16)] + [pltpu.SemaphoreType.DMA((n,)) for n in (BOXES, BOXES, MATS)],
+        compiler_params=pltpu.CompilerParams(vmem_limit_bytes=VMEM_FEW),
         name="settle",
-    )(*[pltpu.with_memory_space_constraint(waves[n].reshape(X, *shape), home(n)) for n in SETTLED])
-    return [out.reshape(2, -1, out.shape[-1]) for out in outs]
+    )(*[pltpu.with_memory_space_constraint(waves[n].reshape(shape), home(n)) for n in SETTLED], *grads, *moments, factor)
+    return [out.reshape(2, -1, out.shape[-1]) for out in outs[:3]], outs[3:]
 
 
 def device_step(dims, x, dy, wg, wu, wd, *moments):
-    m, v = moments[:3], moments[3:]
     grads = scatter(factors(x[0], dy[0], wg, wu, wd), dims)
     place = lax.axis_index("dp")
-    w = [lax.dynamic_slice_in_dim(a, place * b.shape[1], b.shape[1], 1) for a, b in zip((wg, wu, wd), m, strict=True)]
-    flip = [jnp.swapaxes(a, 0, 1) for a in (*m, *v)]
-    mv, out = update(grads, w, flip, dims)
-    mv = [jnp.swapaxes(a, 0, 1) for a in mv]
-    return (*settle(out, dims), *mv)
+    w = [lax.dynamic_slice_in_dim(a, place * b.shape[1], b.shape[1], 1) for a, b in zip((wg, wu, wd), moments[:3], strict=True)]
+    moments = [jnp.swapaxes(a, 0, 1) for a in moments]
+    factor, waves = update(grads, w, moments, dims)
+    new, moments = settle(waves, factor, grads, moments, dims)
+    return (*new, *[jnp.swapaxes(a, 0, 1) for a in moments])
 
 
 DIMS = {256: (4, 4, 8)}

time: 580 us -> 548 us (0.945)
  Pallas kernels: 571 us -> 543 us
    pallas_call x1, Pallas kernels: 48.4 us -> 32.6 us  [settle(): pl.pallas_call(lambda *refs: settle_kernel(*refs[:MATS + 2 + len(moments)...]
    pallas_call x3, Pallas kernels: 157 us -> 145 us  [layer_call(): pl.pallas_call(kernel, grid=(FF // WIDTH,), in_specs=[whole] * len(tokens...]
    unnamed x22 -> x0, local copies, waits for them, and re-layouts: 5.87 us -> none
where the time goes in v3:
time: 548 us
  Pallas kernels  543 us (99%)
    pallas_call x1, Pallas kernels, scatter(): pl.pallas_call(functools.partial(scatter_kernel, dims, tuple(scratch)), o...  196 us
    pallas_call x1, Pallas kernels, update(): pl.pallas_call(functools.partial(update_kernel, dims, tuple(scratch)), ou...  169 us
    pallas_call x3, Pallas kernels, layer_call(): pl.pallas_call(kernel, grid=(FF // WIDTH,), in_specs=[whole] * len(tokens...  145 us
    pallas_call x1, Pallas kernels, settle(): pl.pallas_call(lambda *refs: settle_kernel(*refs[:MATS + 2 + len(moments)...  32.6 us

profile of v3, /device:TPU:1, one launch (start us, length us, event | category | flops | bytes accessed | tf_op | source)
XLA Modules:
  0.0 547.6 jit_solution(15807786937322002412)
XLA Ops:
  0.6 1.6 constant_dynamic-slice_fusion.refs_4_
  2.2 1.8 constant_dynamic-slice_fusion.1
  4.0 46.3 %bottom.1 = (bf16[1024,1536]{1,0:T(8,128)(2,1)}, f32[1024,3584]{1,0:T(8,128)}, f32[1024,3584]{1,0:T(8,128)}, bf16[1024,3584]{1,0:T(8,128)(2,1)}, bf16[1024,1536]{1,0:T(8,128)(2,1)}) custom-call(bf16[1024,1536]{1,0:T(8,128)(2,1)} %bitcast.46, bf16[2,1536,3584]{2,1,0:T(8,128)(2,1)} %wg.3, bf16[2,1536,3584]{2,1,0:T(8,128)(2,1)} %wu.3, bf16[2,3584,1536]{2,1,0:T(8,128)(2,1)} %wd.5), custom_call_target="tpu_custom_call" | custom-call | flops 33822867456 | bytes 33030144 | tf_op jit(solution)/shard_map/bottom/pallas_call | solution.py:828
  50.4 72.8 %top.1 = (bf16[1024,1536]{1,0:T(8,128)(2,1)}, bf16[1024,3584]{1,0:T(8,128)(2,1)}, bf16[1024,3584]{1,0:T(8,128)(2,1)}, bf16[1024,3584]{1,0:T(8,128)(2,1)}, bf16[1024,1536]{1,0:T(8,128)(2,1)}) custom-call(bf16[1024,1536]{1,0:T(8,128)(2,1)} %get-tuple-element.39.h, bf16[1024,1536]{1,0:T(8,128)(2,1)} %bitcast.29, bf16[2,1536,3584]{2,1,0:T(8,128)(2,1)} %wg.3, ...), custom_call_target="tpu_custom_call" | custom-call | flops 56371445760 | bytes 33030144 | tf_op jit(solution)/shard_map/top/pallas_call | solution.py:828
  123.2 25.8 %back.1 = (bf16[1024,3584]{1,0:T(8,128)(2,1)}, bf16[1024,3584]{1,0:T(8,128)(2,1)}) custom-call(bf16[1024,1536]{1,0:T(8,128)(2,1)} %get-tuple-element.46.dh.refs_9_, f32[1024,3584]{1,0:T(8,128)} %get-tuple-element.47.gate, f32[1024,3584]{1,0:T(8,128)} %get-tuple-element.48.up, bf16[2,3584,1536]{2,1,0:T(8,128)(2,1)} %wd.5), custom_call_target="tpu_custom_call" | custom-call | flops 11274289152 | bytes 11010048 | tf_op jit(solution)/shard_map/back/pallas_call | solution.py:828
  149.0 196.4 %scatter.1 = (bf16[4,8,3584]{2,1,0:T(8,128)(2,1)}, bf16[2,16,1536]{2,1,0:T(8,128)(2,1)}, bf16[6,4,4,8,24,896]{5,4,3,2,1,0:T(8,128)(2,1)}, bf16[6,4,4,8,24,896]{5,4,3,2,1,0:T(8,128)(2,1)}) custom-call(bf16[1024,3584]{1,0:T(8,128)(2,1)} %get-tuple-element.40.refs_0_, bf16[1024,1536]{1,0:T(8,128)(2,1)} %get-tuple-element.41.refs_1_.refs_2_, ...), custom_call_target="tpu_custom_call" | custom-call | tf_op jit(solution)/shard_map/scatter/pallas_call | solution.py:502
  345.4 169.4 %update.1 = (f32[8,128]{1,0:T(8,128)}, bf16[4,4,8,2,24,896]{5,4,3,2,1,0:T(8,128)(2,1)S(1)}, bf16[4,4,8,2,24,896]{5,4,3,2,1,0:T(8,128)(2,1)S(1)}, bf16[4,4,8,2,24...) custom-call(bf16[4,8,3584]{2,1,0:T(8,128)(2,1)} %get-tuple-element.5, ...), custom_call_target="tpu_custom_call" | custom-call | tf_op jit(solution)/shard_map/update/pallas_call | solution.py:701
  514.8 32.6 %settle.1 = (bf16[2,4,4,4,24,3584]{5,4,3,2,1,0:T(8,128)(2,1)}, bf16[2,4,4,4,24,3584]{5,4,3,2,1,0:T(8,128)(2,1)}, bf16[2,4,4,4,56,1536]{5,4,3,2,1,0:T(8,128)(2,1)...) custom-call(bf16[4,4,4,2,2,24,896]{6,5,4,3,2,1,0:T(8,128)(2,1)} %bit, ...), custom_call_target="tpu_custom_call" | custom-call | tf_op jit(solution)/shard_map/settle/pallas_call | solution.py:919

commit v4 on v3

--- a/solution.py
+++ b/solution.py
@@ -13,8 +13,8 @@
 ORDERS = ("xyz", "yzx", "zxy")
 COLUMNS = ((0, 384), (384, 256), (640, 256))
 KINDS = ("s", "f", "z", "d", "e")
-SCATTER_TIMES = '$*115::B$)-.24688;;A$()+//336<<A'
-GATHER_TIMES, GATHER_STEPS = '#-.4799Yj~#337;<DEOPQ_oi#((3@AAKX\\bgoy', (4, 14)
+SCATTER_TIMES = '$*115::B$)-/12479;;A$()+-0339<<A'
+GATHER_TIMES, GATHER_STEPS = '$119???`j~$44>>EEQRYYeoo#))2IIISZ`ijxx', (4, 14)
 MESH = pl.DeviceIdType.MESH
 START, MORE = 0, 1
 NORTH, SOUTH = 0, 1

time: 548 us -> 542 us (0.989)
  no operation moved by 1% of the time
where the time goes in v4:
time: 542 us
  Pallas kernels  538 us (99%)
    pallas_call x1, Pallas kernels, scatter(): pl.pallas_call(functools.partial(scatter_kernel, dims, tuple(scratch)), o...  194 us
    pallas_call x1, Pallas kernels, update(): pl.pallas_call(functools.partial(update_kernel, dims, tuple(scratch)), ou...  167 us
    pallas_call x3, Pallas kernels, layer_call(): pl.pallas_call(kernel, grid=(FF // WIDTH,), in_specs=[whole] * len(tokens...  145 us
    pallas_call x1, Pallas kernels, settle(): pl.pallas_call(lambda *refs: settle_kernel(*refs[:MATS + 2 + len(moments)...  32.6 us

profile of v4, /device:TPU:1, one launch (start us, length us, event | category | flops | bytes accessed | tf_op | source)
XLA Modules:
  0.0 542.1 jit_solution(14003305952309212129)
XLA Ops:
  0.6 1.6 constant_dynamic-slice_fusion.refs_4_
  2.2 1.8 constant_dynamic-slice_fusion.1
  4.0 46.3 %bottom.1 = (bf16[1024,1536]{1,0:T(8,128)(2,1)}, f32[1024,3584]{1,0:T(8,128)}, f32[1024,3584]{1,0:T(8,128)}, bf16[1024,3584]{1,0:T(8,128)(2,1)}, bf16[1024,1536]{1,0:T(8,128)(2,1)}) custom-call(bf16[1024,1536]{1,0:T(8,128)(2,1)} %bitcast.46, bf16[2,1536,3584]{2,1,0:T(8,128)(2,1)} %wg.3, bf16[2,1536,3584]{2,1,0:T(8,128)(2,1)} %wu.3, bf16[2,3584,1536]{2,1,0:T(8,128)(2,1)} %wd.5), custom_call_target="tpu_custom_call" | custom-call | flops 33822867456 | bytes 33030144 | tf_op jit(solution)/shard_map/bottom/pallas_call | solution.py:828
  50.4 72.8 %top.1 = (bf16[1024,1536]{1,0:T(8,128)(2,1)}, bf16[1024,3584]{1,0:T(8,128)(2,1)}, bf16[1024,3584]{1,0:T(8,128)(2,1)}, bf16[1024,3584]{1,0:T(8,128)(2,1)}, bf16[1024,1536]{1,0:T(8,128)(2,1)}) custom-call(bf16[1024,1536]{1,0:T(8,128)(2,1)} %get-tuple-element.39.h, bf16[1024,1536]{1,0:T(8,128)(2,1)} %bitcast.29, bf16[2,1536,3584]{2,1,0:T(8,128)(2,1)} %wg.3, ...), custom_call_target="tpu_custom_call" | custom-call | flops 56371445760 | bytes 33030144 | tf_op jit(solution)/shard_map/top/pallas_call | solution.py:828
  123.2 25.8 %back.1 = (bf16[1024,3584]{1,0:T(8,128)(2,1)}, bf16[1024,3584]{1,0:T(8,128)(2,1)}) custom-call(bf16[1024,1536]{1,0:T(8,128)(2,1)} %get-tuple-element.46.dh.refs_9_, f32[1024,3584]{1,0:T(8,128)} %get-tuple-element.47.gate, f32[1024,3584]{1,0:T(8,128)} %get-tuple-element.48.up, bf16[2,3584,1536]{2,1,0:T(8,128)(2,1)} %wd.5), custom_call_target="tpu_custom_call" | custom-call | flops 11274289152 | bytes 11010048 | tf_op jit(solution)/shard_map/back/pallas_call | solution.py:828
  149.0 193.6 %scatter.1 = (bf16[4,8,3584]{2,1,0:T(8,128)(2,1)}, bf16[2,16,1536]{2,1,0:T(8,128)(2,1)}, bf16[6,4,4,8,24,896]{5,4,3,2,1,0:T(8,128)(2,1)}, bf16[6,4,4,8,24,896]{5,4,3,2,1,0:T(8,128)(2,1)}) custom-call(bf16[1024,3584]{1,0:T(8,128)(2,1)} %get-tuple-element.40.refs_0_, bf16[1024,1536]{1,0:T(8,128)(2,1)} %get-tuple-element.41.refs_1_.refs_2_, ...), custom_call_target="tpu_custom_call" | custom-call | tf_op jit(solution)/shard_map/scatter/pallas_call | solution.py:502
  342.6 166.8 %update.1 = (f32[8,128]{1,0:T(8,128)}, bf16[4,4,8,2,24,896]{5,4,3,2,1,0:T(8,128)(2,1)S(1)}, bf16[4,4,8,2,24,896]{5,4,3,2,1,0:T(8,128)(2,1)S(1)}, bf16[4,4,8,2,24...) custom-call(bf16[4,8,3584]{2,1,0:T(8,128)(2,1)} %get-tuple-element.5, ...), custom_call_target="tpu_custom_call" | custom-call | tf_op jit(solution)/shard_map/update/pallas_call | solution.py:701
  509.4 32.6 %settle.1 = (bf16[2,4,4,4,24,3584]{5,4,3,2,1,0:T(8,128)(2,1)}, bf16[2,4,4,4,24,3584]{5,4,3,2,1,0:T(8,128)(2,1)}, bf16[2,4,4,4,56,1536]{5,4,3,2,1,0:T(8,128)(2,1)...) custom-call(bf16[4,4,4,2,2,24,896]{6,5,4,3,2,1,0:T(8,128)(2,1)} %bit, ...), custom_call_target="tpu_custom_call" | custom-call | tf_op jit(solution)/shard_map/settle/pallas_call | solution.py:919
